TPU v7x, 256 devices: a 8x8x2 block of a 8x8x16 slice. The times are simulated.
256 devices in a mesh: stripe: 2 (over z), row: 64 (over x, y), col: 2 (over core).
Axes of the slice: x: 8, y: 8, z: 2, core: 2. Of those that a mesh axis runs over, the one named last changes fastest.
The devices are a block of a 8x8x16 slice.
Arguments:
- coverage: int32 [32768, 4096], P(('stripe', 'row'), 'col'), parts along dimension 0, may hold values from 0 to 255
- fog_rows: float32 [64, 64], replicated, may hold values from 0.02 to 50
- fog_cols: float32 [16, 16], replicated, may hold values from 0.02 to 50
Outputs:
- dose: float32 [32768, 4096], P(('stripe', 'row'), 'col'), parts along dimension 0
There are 2 independent parts, one for each index of `stripe`. A program takes and returns all parts, laid end to end along the dimension named above; an argument that names none is the same for every part. Nothing has to cross between parts.
All inputs are finite; a program needn't handle non-finite values.
Results may differ from a plain program's by a relative error of at most 0.0001.
Values sent between devices are 32-bit elements; how exact they have to be, the bound alone decides.
A program may use at most 64 MiB of HBM per device.

v0:
```python
import math

import jax
import jax.numpy as jnp
from jax import lax
from jax.sharding import Mesh
from jax.sharding import PartitionSpec as P

BS = 32
FB = 256
HALO = 4
BSIG = 16
REACH = 40
PASSES = 2
ROW = ("row_0", "row_1")
STRIPE_ROW = ("stripe", "row_0", "row_1")


def extended(value, sides, width):
    for axis, dim in sides:
        count, length = (lax.axis_size(axis), value.shape[dim])
        up = [(i, (i + 1) % count) for i in range(count - 1)]
        down = [(j, i) for i, j in up]
        last = lax.slice_in_dim(value, length - width, length, axis=dim)
        initial = lax.slice_in_dim(value, 0, width, axis=dim)
        before = lax.ppermute(last, axis, up)
        after = lax.ppermute(initial, axis, down)
        value = jnp.concatenate([before, value, after], axis=dim)
    return value


def from_everyone(value, axis):
    count = lax.axis_size(axis)
    return lax.all_to_all(
        jnp.broadcast_to(value[None], (count, *value.shape)), axis, 0, 0, tiled=True
    )


def laid_out(tiles, dim):
    tiles = jnp.moveaxis(tiles, 0, dim)
    shape = tiles.shape
    return tiles.reshape(*shape[:dim], shape[dim] * shape[dim + 1], *shape[dim + 2 :])


def gather_axes(value, axes, dim):
    far, near = axes
    initial = from_everyone(value, far)
    tiles = jnp.swapaxes(from_everyone(initial, near), 0, 1)
    return laid_out(tiles.reshape(-1, *value.shape), dim)


def fine_taps():
    offsets = jnp.arange(-HALO, HALO + 1).astype(jnp.float32)
    raw = jnp.exp(-0.5 * (offsets / 1.25) ** 2)
    return raw / jnp.sum(raw)


def blur_padded(padded, rows, cols):
    taps = fine_taps()
    across = taps[0] * padded[0:rows, :]
    for index in range(1, 2 * HALO + 1):
        across = across + taps[index] * padded[index : index + rows, :]
    result = taps[0] * across[:, 0:cols]
    for index in range(1, 2 * HALO + 1):
        result = result + taps[index] * across[:, index : index + cols]
    return result


def block_mean(field, size):
    rows, cols = field.shape
    return field.reshape(rows // size, size, cols // size, size).sum(axis=(1, 3)) / (size * size)


def spread_add(field, small, size, weight):
    rows, cols = field.shape
    return (
        field.reshape(rows // size, size, cols // size, size) + weight * small[:, None, :, None]
    ).reshape(rows, cols)


def gauss_matrix(first, second):
    offsets = (first[:, None] - second[None, :]).astype(jnp.float32)
    values = jnp.exp(-0.5 * (offsets / BSIG) ** 2) / (BSIG * math.sqrt(2.0 * math.pi))
    return jnp.where(jnp.abs(offsets) <= REACH, values, jnp.zeros_like(values))


def shards(coverage, fog_rows, fog_cols):
    high = lax.Precision.HIGHEST
    cover = coverage.astype(jnp.float32) / 255.0
    rows, cols = cover.shape
    dose = jnp.ones((rows, cols), jnp.float32)
    row_place = lax.axis_index(ROW)
    col_place = lax.axis_index("col")
    row_count = lax.axis_size(ROW)
    col_count = lax.axis_size("col")
    back_rows = rows // BS
    back_cols = cols // BS
    fog_here_rows = rows // FB
    fog_here_cols = cols // FB
    row_norm = fog_rows / jnp.sum(fog_rows, axis=1, keepdims=True)
    col_norm = fog_cols / jnp.sum(fog_cols, axis=1, keepdims=True)
    row_norm_own = lax.dynamic_slice_in_dim(row_norm, row_place * fog_here_rows, fog_here_rows, 0)
    col_norm_own = lax.dynamic_slice_in_dim(col_norm, col_place * fog_here_cols, fog_here_cols, 0)
    all_back_cols = back_cols * col_count
    all_back_rows = back_rows * row_count
    own_back_cols = col_place * back_cols + jnp.arange(back_cols, dtype=jnp.int32)
    own_back_rows = row_place * back_rows + jnp.arange(back_rows, dtype=jnp.int32)
    across_gauss = gauss_matrix(jnp.arange(all_back_cols, dtype=jnp.int32), own_back_cols)
    for step in range(PASSES):
        charge = dose * cover
        padded = extended(charge, ((ROW, 0), ("col", 1)), HALO)
        fine = blur_padded(padded, rows, cols)
        back = block_mean(charge, BS)
        stacked = gather_axes(back, (("row_0", "row_1"), "col"), 0)
        back_all = (
            stacked.reshape(row_count, col_count, back_rows, back_cols)
            .transpose(0, 2, 1, 3)
            .reshape(all_back_rows, all_back_cols)
        )
        back_h_all = jnp.dot(back_all, across_gauss, precision=high)
        down_own = gauss_matrix(own_back_rows, jnp.arange(all_back_rows, dtype=jnp.int32))
        back_v = jnp.dot(down_own, back_h_all, precision=high)
        fogmean = block_mean(back_all, FB // BS)
        fog = jnp.dot(
            jnp.dot(row_norm_own, fogmean, precision=high), col_norm_own.T, precision=high
        )
        energy = spread_add(fine, back_v, BS, 0.6)
        energy = spread_add(energy, fog, FB, 0.4) / 2.0
        dose = dose + (0.5 - energy)
    return dose


def solution(mesh):
    split = Mesh(
        mesh.devices.reshape(mesh.shape["stripe"], 8, 8, mesh.shape["col"]),
        ("stripe", "row_0", "row_1", "col"),
    )
    placed = (P(STRIPE_ROW, "col"), P(), P())
    return jax.shard_map(
        shards, mesh=split, in_specs=placed, out_specs=P(STRIPE_ROW, "col"), check_vma=False
    )
```

profile of v0, /device:TPU:513, one launch (start us, length us, event | category | flops | bytes accessed | tf_op | source)
XLA Modules:
  0.0 183.4 jit_solution(5561155043255975465)
XLA Ops:
  0.0 1.8 convert_multiply_fusion
  1.8 5.3 %collective-permute-start = (f32[4,2048]{1,0:T(4,128)S(1)}, f32[4,2048]{1,0:T(4,128)S(1)}, u32[]{:S(2)}, u32[]{:S(2)}) collective-permute-start(f32[4,2048]{1,0:T(4,128)S(1)} %get-tuple-element.13), channel_id=1, source_target_pairs={{0,2},{2,4},{4,6},{6,8},{8,10},{10,12},{12,14},{14,16},{16,18},{18... | collective-permute-start | bytes 98312 | tf_op jit(solution)/shard_map/ppermute | solution.py:26
  7.1 1.3 collective-permute-start.1
  8.4 4.8 %reshape.78 = f32[8,32,64,32]{3,2,1,0:T(8,128)} reshape(f32[256,2048]{1,0:T(8,128)S(1)} %convert_multiply_fusion) | data formatting | bytes 4194304 | tf_op jit(solution)/shard_map/reshape | solution.py:71
  13.2 4.2 %reduce_sum.82 = f32[8,64]{1,0:T(8,128)S(1)} reduce(f32[8,32,64,32]{3,2,1,0:T(8,128)} %reshape.78, f32[]{:T(128)} %constant.25.clone.1), dimensions={1,3}, to_apply=%region_1.0 | reduce | flops 523776 | bytes 2099204 | tf_op jit(solution)/shard_map/reduce_sum | solution.py:71
  17.4 0.8 reshape.91
  18.2 20.6 %all-to-all-start = ((f32[64,1,512]{2,1,0:T(1,128)}), f32[64,1,512]{2,1,0:T(1,128)S(1)}, u32[]{:S(2)}, u32[]{:S(2)}) async-start(f32[64,1,512]{2,1,0:T(1,128)} %reshape.91), calls=%async_computation | async-start | bytes 262144 | tf_op jit(solution)/shard_map/all_to_all | solution.py:34
  38.8 0.7 fusion.75
  39.5 0.7 broadcast_divide_fusion
  40.2 0.7 fusion.104
  41.0 0.2 pad_maximum_fusion
  41.2 1.3 copy-done.4
  42.6 4.4 %collective-permute-start.3 = (f32[264,4]{1,0:T(8,128)S(1)}, f32[264,4]{1,0:T(8,128)S(1)}, u32[]{:S(2)}, u32[]{:S(2)}) collective-permute-start(f32[264,4]{1,0:T(8,128)S(1)} %get-tuple-element.9), channel_id=1, source_target_pairs={{1,0},{3,2},{5,4},{7,6},{9,8},{11,10},{13,12},{15,14},{17,16},{19,... | collective-permute-start | bytes 12680 | tf_op jit(solution)/shard_map/ppermute | solution.py:27
  47.1 1.3 collective-permute-start.2
  48.4 0.1 reduce_sum.83
  48.5 0.1 reduce_sum.87
  48.6 0.7 dynamic-slice
  49.4 1.0 collective-permute-done.2
  50.3 3.0 %concatenate.13 = f32[264,2056]{1,0:T(8,128)S(1)} concatenate(f32[264,4]{1,0:T(8,128)S(1)} %collective-permute-done.2, f32[264,2048]{1,0:T(8,128)} %copy-done.4, f32[264,4]{1,0:T(8,128)S(1)} %collective-permute-done.3), dimensions={1} | concatenate | bytes 4342272 | tf_op jit(solution)/shard_map/concatenate | solution.py:28
  53.4 8.8 %fusion.8 = f32[256,2056]{1,0:T(8,128)} fusion(f32[264,2056]{1,0:T(8,128)S(1)} %concatenate.13, f32[]{:T(128)} %bitcast.8, f32[]{:T(128)} %bitcast.7, f32[]{:T(128)} %bitcast.6, f32[]{:T(128)} %bitcast.5, f32[]{:T(128)} %bitcast.4, f32[]{:T(128)} %bitcast.3, f32[]{:T(128)} %bitcast.2, f32[]{:T(128)} %bitcast.1, f32[]{:T(128)} %bitcast), kind=kLoop, calls=%fused_computation.18 | loop fusion | flops 8947712 | bytes 21053476 | tf_op jit(solution)/shard_map/add | solution.py:62
  62.1 0.5 broadcast.178
  62.7 0.9 reduce.4
  63.7 0.3 reshape.93
  64.1 3.9 %all_to_all.20 = f32[2,1,32768]{2,1,0:T(1,128)S(1)} all-to-all(f32[2,1,32768]{2,1,0:T(1,128)S(1)} %reshape.93), channel_id=1, replica_groups=mesh['stripe'=2,'row_0'=8,'row_1'=8,'col'=2] {'col'}, dimensions={0} | all-to-all | bytes 524288 | tf_op jit(solution)/shard_map/all_to_all | solution.py:34
  67.9 1.4 reduce.5
  69.3 0.3 reshape.94
  69.7 0.2 bitcast_reduce_fusion.1
  70.0 0.8 convolution_bitcast_fusion.3
  70.8 0.2 fusion.41
  71.1 0.4 copy.4
  71.5 0.3 reshape.79
  71.8 0.4 fusion.44
  72.2 0.2 convolution_multiply_fusion.1
  72.5 4.4 %add.213 = f32[8,32,64,32]{3,2,1,0:T(8,128)} broadcast(f32[8,64]{1,0:T(8,128)S(1)} %convolution_multiply_fusion.1), dimensions={0,2} | broadcast | bytes 2099200 | tf_op jit(solution)/shard_map/add | solution.py:77
  76.9 7.6 %add.214 = f32[256,2048]{1,0:T(8,128)} reshape(f32[8,32,64,32]{3,2,1,0:T(8,128)} %add.213) | data formatting | bytes 4194304 | tf_op jit(solution)/shard_map/add | solution.py:77
  84.5 12.5 %fusion.98 = (f32[256,2048]{1,0:T(8,128)S(1)}, f32[256,2048]{1,0:T(8,128)}) fusion(s32[256,2048]{1,0:T(8,128)} %param.3, f32[2048]{0:T(1024)S(1)} %bitcast.57, f32[256,2048]{1,0:T(8,128)} %add.214, f32[256,2056]{1,0:T(8,128)S(1)} %copy-done.1, f32[]{:T(128)} %bitcast.8, f32[]{:T(128)} %bitcast.7, f32[]{:T(128)} %bitcast.6, f32[]{:T(128)} %bitcast.5, ...), kind=kLoop, calls=%fused_computation.159 | loop fusion | flops 12582912 | bytes 27271204 | tf_op jit(solution)/shard_map/mul | solution.py:110
  97.1 1.4 copy-done.2
  98.5 3.0 %collective-permute-start.4 = (f32[4,2048]{1,0:T(4,128)S(1)}, f32[4,2048]{1,0:T(4,128)S(1)}, u32[]{:S(2)}, u32[]{:S(2)}) collective-permute-start(f32[4,2048]{1,0:T(4,128)S(1)} %get-tuple-element.11), channel_id=1, source_target_pairs={{0,2},{2,4},{4,6},{6,8},{8,10},{10,12},{12,14},{14,16},{16,18},{18... | collective-permute-start | bytes 98312 | tf_op jit(solution)/shard_map/ppermute | solution.py:26
  101.5 1.3 collective-permute-start.5
  102.8 6.3 %reshape.81 = f32[8,32,64,32]{3,2,1,0:T(8,128)} reshape(f32[256,2048]{1,0:T(8,128)} %copy-done.2) | data formatting | bytes 4194304 | tf_op jit(solution)/shard_map/reshape | solution.py:71
  109.0 4.3 %reduce_sum.88 = f32[8,64]{1,0:T(8,128)S(1)} reduce(f32[8,32,64,32]{3,2,1,0:T(8,128)} %reshape.81, f32[]{:T(128)} %constant.25.clone.1), dimensions={1,3}, to_apply=%region_6.7 | reduce | flops 523776 | bytes 2099204 | tf_op jit(solution)/shard_map/reduce_sum | solution.py:71
  113.4 0.2 pad_maximum_fusion.1
  113.6 1.3 copy-done.5
  115.1 2.5 %collective-permute-start.7 = (f32[264,4]{1,0:T(8,128)S(1)}, f32[264,4]{1,0:T(8,128)S(1)}, u32[]{:S(2)}, u32[]{:S(2)}) collective-permute-start(f32[264,4]{1,0:T(8,128)S(1)} %get-tuple-element.7), channel_id=1, source_target_pairs={{1,0},{3,2},{5,4},{7,6},{9,8},{11,10},{13,12},{15,14},{17,16},{19,... | collective-permute-start | bytes 12680 | tf_op jit(solution)/shard_map/ppermute | solution.py:27
  117.6 1.3 collective-permute-start.6
  118.9 0.8 reshape.95
  119.8 16.2 %all-to-all-start.2 = ((f32[64,1,512]{2,1,0:T(1,128)}), f32[64,1,512]{2,1,0:T(1,128)S(1)}, u32[]{:S(2)}, u32[]{:S(2)}) async-start(f32[64,1,512]{2,1,0:T(1,128)} %reshape.95), calls=%async_computation.2 | async-start | bytes 262144 | tf_op jit(solution)/shard_map/all_to_all | solution.py:34
  136.0 3.0 %concatenate.15 = f32[264,2056]{1,0:T(8,128)S(1)} concatenate(f32[264,4]{1,0:T(8,128)S(1)} %collective-permute-done.6, f32[264,2048]{1,0:T(8,128)} %copy-done.5, f32[264,4]{1,0:T(8,128)S(1)} %collective-permute-done.7), dimensions={1} | concatenate | bytes 4342272 | tf_op jit(solution)/shard_map/concatenate | solution.py:28
  139.0 8.8 %fusion = f32[256,2056]{1,0:T(8,128)} fusion(f32[264,2056]{1,0:T(8,128)S(1)} %concatenate.15, f32[]{:T(128)} %bitcast.8, f32[]{:T(128)} %bitcast.7, f32[]{:T(128)} %bitcast.6, f32[]{:T(128)} %bitcast.5, f32[]{:T(128)} %bitcast.4, f32[]{:T(128)} %bitcast.3, f32[]{:T(128)} %bitcast.2, f32[]{:T(128)} %bitcast.1, f32[]{:T(128)} %bitcast), kind=kLoop, calls=%fused_computation.1 | loop fusion | flops 8947712 | bytes 21053476 | tf_op jit(solution)/shard_map/add | solution.py:62
  147.8 0.9 reduce.6
  148.9 0.3 reshape.97
  149.2 5.0 %all_to_all.21 = f32[2,1,32768]{2,1,0:T(1,128)S(1)} all-to-all(f32[2,1,32768]{2,1,0:T(1,128)S(1)} %reshape.97), channel_id=1, replica_groups=mesh['stripe'=2,'row_0'=8,'row_1'=8,'col'=2] {'col'}, dimensions={0} | all-to-all | bytes 524288 | tf_op jit(solution)/shard_map/all_to_all | solution.py:34
  154.2 1.4 reduce.7
  155.6 0.3 reshape.98
  156.0 0.2 bitcast_reduce_fusion
  156.3 0.8 convolution_bitcast_fusion.1
  157.1 0.2 fusion.42
  157.4 0.4 copy.7
  157.8 0.3 reshape.82
  158.1 0.4 fusion.43
  158.5 0.2 convolution_multiply_fusion
  158.8 4.4 %add.238 = f32[8,32,64,32]{3,2,1,0:T(8,128)} broadcast(f32[8,64]{1,0:T(8,128)S(1)} %convolution_multiply_fusion), dimensions={0,2} | broadcast | bytes 2099200 | tf_op jit(solution)/shard_map/add | solution.py:77
  163.2 7.7 %add.239 = f32[256,2048]{1,0:T(8,128)} reshape(f32[8,32,64,32]{3,2,1,0:T(8,128)} %add.238) | data formatting | bytes 4194304 | tf_op jit(solution)/shard_map/add | solution.py:77
  170.8 12.5 %fusion.21 = f32[256,2048]{1,0:T(8,128)} fusion(f32[256,2048]{1,0:T(8,128)} %get-tuple-element.6, f32[256,2048]{1,0:T(8,128)} %add.239, f32[256,2056]{1,0:T(8,128)S(1)} %copy-done, f32[2048]{0:T(1024)S(1)} %bitcast.56, f32[]{:T(128)} %bitcast.8, f32[]{:T(128)} %bitcast.7, f32[]{:T(128)} %bitcast.6, f32[]{:T(128)} %bitcast.5, f32[]{:T(128)} %bitcast.4, ...), kind=kLoop, calls=%fused_computation.42 | loop fusion | flops 11534336 | bytes 25174052 | tf_op jit(solution)/shard_map/add | solution.py:129
  (45 shorter events, 1.0 us)
Async XLA Ops:
  1.8 39.1 %collective-permute-start = (f32[4,2048]{1,0:T(4,128)S(1)}, f32[4,2048]{1,0:T(4,128)S(1)}, u32[]{:S(2)}, u32[]{:S(2)}) collective-permute-start(f32[4,2048]{1,0:T(4,128)S(1)} %get-tuple-element.13), channel_id=1, source_target_pairs={{0,2},{2,4},{4,6},{6,8},{8,10},{10,12},{12,14},{14,16},{16,18},{18... | collective-permute-start | bytes 98312 | tf_op jit(solution)/shard_map/ppermute | solution.py:26
  7.1 33.9 %collective-permute-start.1 = (f32[4,2048]{1,0:T(4,128)S(1)}, f32[4,2048]{1,0:T(4,128)S(1)}, u32[]{:S(2)}, u32[]{:S(2)}) collective-permute-start(f32[4,2048]{1,0:T(4,128)S(1)} %get-tuple-element.14), channel_id=1, source_target_pairs={{2,0},{4,2},{6,4},{8,6},{10,8},{12,10},{14,12},{16,14},{18,16},{20... | collective-permute-start | bytes 98312 | tf_op jit(solution)/shard_map/ppermute | solution.py:27
  18.2 43.9 %all-to-all-start = ((f32[64,1,512]{2,1,0:T(1,128)}), f32[64,1,512]{2,1,0:T(1,128)S(1)}, u32[]{:S(2)}, u32[]{:S(2)}) async-start(f32[64,1,512]{2,1,0:T(1,128)} %reshape.91), calls=%async_computation | async-start | bytes 262144 | tf_op jit(solution)/shard_map/all_to_all | solution.py:34
  40.9 7.5 %copy-start.6 = (f32[64,64]{1,0:T(8,128)S(1)}, f32[64,64]{1,0:T(8,128)}, u32[]{:S(2)}) copy-start(f32[64,64]{1,0:T(8,128)} %param.4) | copy-start | bytes 49156
  40.9 7.6 %copy-start.7 = (f32[16,16]{1,0:T(8,128)S(1)}, f32[16,16]{1,0:T(8,128)}, u32[]{:S(2)}) copy-start(f32[16,16]{1,0:T(8,128)} %param.5) | copy-start | bytes 3076
  41.2 1.4 copy-start.4
  42.6 6.7 %collective-permute-start.3 = (f32[264,4]{1,0:T(8,128)S(1)}, f32[264,4]{1,0:T(8,128)S(1)}, u32[]{:S(2)}, u32[]{:S(2)}) collective-permute-start(f32[264,4]{1,0:T(8,128)S(1)} %get-tuple-element.9), channel_id=1, source_target_pairs={{1,0},{3,2},{5,4},{7,6},{9,8},{11,10},{13,12},{15,14},{17,16},{19,... | collective-permute-start | bytes 12680 | tf_op jit(solution)/shard_map/ppermute | solution.py:27
  47.1 3.3 %collective-permute-start.2 = (f32[264,4]{1,0:T(8,128)S(1)}, f32[264,4]{1,0:T(8,128)S(1)}, u32[]{:S(2)}, u32[]{:S(2)}) collective-permute-start(f32[264,4]{1,0:T(8,128)S(1)} %get-tuple-element.10), channel_id=1, source_target_pairs={{0,1},{2,3},{4,5},{6,7},{8,9},{10,11},{12,13},{14,15},{16,17},{18,... | collective-permute-start | bytes 12680 | tf_op jit(solution)/shard_map/ppermute | solution.py:26
  76.9 7.7 %copy-start.1 = (f32[256,2056]{1,0:T(8,128)S(1)}, f32[256,2056]{1,0:T(8,128)}, u32[]{:S(2)}) copy-start(f32[256,2056]{1,0:T(8,128)} %fusion.8) | copy-start | bytes 6316036
  97.1 1.4 copy-start.2
  98.5 14.9 %collective-permute-start.4 = (f32[4,2048]{1,0:T(4,128)S(1)}, f32[4,2048]{1,0:T(4,128)S(1)}, u32[]{:S(2)}, u32[]{:S(2)}) collective-permute-start(f32[4,2048]{1,0:T(4,128)S(1)} %get-tuple-element.11), channel_id=1, source_target_pairs={{0,2},{2,4},{4,6},{6,8},{8,10},{10,12},{12,14},{14,16},{16,18},{18... | collective-permute-start | bytes 98312 | tf_op jit(solution)/shard_map/ppermute | solution.py:26
  101.5 11.9 %collective-permute-start.5 = (f32[4,2048]{1,0:T(4,128)S(1)}, f32[4,2048]{1,0:T(4,128)S(1)}, u32[]{:S(2)}, u32[]{:S(2)}) collective-permute-start(f32[4,2048]{1,0:T(4,128)S(1)} %get-tuple-element.12), channel_id=1, source_target_pairs={{2,0},{4,2},{6,4},{8,6},{10,8},{12,10},{14,12},{16,14},{18,16},{20... | collective-permute-start | bytes 98312 | tf_op jit(solution)/shard_map/ppermute | solution.py:27
  109.0 4.3 %copy-start.3 = (f32[256,2048]{1,0:T(8,128)S(1)}, f32[256,2048]{1,0:T(8,128)}, u32[]{:S(2)}) copy-start(f32[256,2048]{1,0:T(8,128)} %copy-done.2) | copy-start | bytes 6291460
  113.6 1.4 copy-start.5
  115.1 20.9 %collective-permute-start.7 = (f32[264,4]{1,0:T(8,128)S(1)}, f32[264,4]{1,0:T(8,128)S(1)}, u32[]{:S(2)}, u32[]{:S(2)}) collective-permute-start(f32[264,4]{1,0:T(8,128)S(1)} %get-tuple-element.7), channel_id=1, source_target_pairs={{1,0},{3,2},{5,4},{7,6},{9,8},{11,10},{13,12},{15,14},{17,16},{19,... | collective-permute-start | bytes 12680 | tf_op jit(solution)/shard_map/ppermute | solution.py:27
  117.6 18.4 %collective-permute-start.6 = (f32[264,4]{1,0:T(8,128)S(1)}, f32[264,4]{1,0:T(8,128)S(1)}, u32[]{:S(2)}, u32[]{:S(2)}) collective-permute-start(f32[264,4]{1,0:T(8,128)S(1)} %get-tuple-element.8), channel_id=1, source_target_pairs={{0,1},{2,3},{4,5},{6,7},{8,9},{10,11},{12,13},{14,15},{16,17},{18,... | collective-permute-start | bytes 12680 | tf_op jit(solution)/shard_map/ppermute | solution.py:26
  119.8 28.0 %all-to-all-start.2 = ((f32[64,1,512]{2,1,0:T(1,128)}), f32[64,1,512]{2,1,0:T(1,128)S(1)}, u32[]{:S(2)}, u32[]{:S(2)}) async-start(f32[64,1,512]{2,1,0:T(1,128)} %reshape.95), calls=%async_computation.2 | async-start | bytes 262144 | tf_op jit(solution)/shard_map/all_to_all | solution.py:34
  163.2 7.7 %copy-start = (f32[256,2056]{1,0:T(8,128)S(1)}, f32[256,2056]{1,0:T(8,128)}, u32[]{:S(2)}) copy-start(f32[256,2056]{1,0:T(8,128)} %fusion) | copy-start | bytes 6316036
where the time goes:
time: 185 us; the launch traced here: 183 us
  other arithmetic  60 us (32%)
  starting transfers between devices  57.2 us (31%)
  local copies, waits for them, and re-layouts  52.5 us (28%)
  blocking collectives  8.87 us (5%)
  matrix products  3.4 us (2%)
    all_to_all x2, starting transfers between devices, from_everyone(): lax.all_to_all(jnp.broadcast_to(value[None], (count, *value.shape)), axis...  36.8 us
    add x4, local copies, waits for them, and re-layouts, spread_add(): field.reshape(rows // size, size, cols // size, size)  24.1 us
    add x2, other arithmetic, blur_padded(): across = across + taps[index] * padded[index:index + rows, :]  17.5 us
    add x1, other arithmetic, shards(): dose = dose + (0.5 - energy)  12.5 us
    mul x1, other arithmetic, shards(): charge = dose * cover  12.5 us
    reshape x2, local copies, waits for them, and re-layouts, block_mean(): field.reshape(rows // size, size, cols // size, size).sum(axis=(1, 3))  11.1 us
    ppermute x4, starting transfers between devices, extended(): before = lax.ppermute(last, axis, up)  10.9 us
    ppermute x4, starting transfers between devices, extended(): after = lax.ppermute(initial, axis, down)  9.56 us
  transfers between devices with their start and end apart: 10, of which 1 were waited for; matrix products, arithmetic and copies ran while one was open for 26% of the time, Pallas kernels for 0%

commit v1 on v0

v1 whole, which is shorter than its diff:
```python
import math

import jax
import jax.numpy as jnp
from jax import lax
from jax.experimental import pallas as pl
from jax.experimental.pallas import tpu as pltpu
from jax.sharding import PartitionSpec as P

BS = 32
FB = 256
HALO = 4
BSIG = 16
REACH = 40
SIDE = 8
MESH = pl.DeviceIdType.MESH
F32 = jnp.float32
BF16 = jnp.bfloat16
I32 = jnp.int32
ORDER = (4, 3, 5, 2, 6, 1, 7)

TAPS = [math.exp(-(k * k) / (2 * 1.25**2)) for k in range(-HALO, HALO + 1)]
TAP_SCALE = 1.0 / sum(TAPS)
GAUSS_SCALE = 1.0 / (BSIG * math.sqrt(2.0 * math.pi))


def iota(shape, dim):
    return lax.broadcasted_iota(I32, shape, dim)


def onehot(condition):
    return jnp.where(condition, 1.0, 0.0).astype(F32)


def taps_of(offset):
    square = (offset * offset).astype(F32)
    value = jnp.exp(square * (-1.0 / (2 * 1.25**2))) * TAP_SCALE
    return jnp.where(jnp.abs(offset) <= HALO, value, 0.0)


def gauss_of(offset):
    square = (offset * offset).astype(F32)
    value = jnp.exp(square * (-0.5 / (BSIG * BSIG))) * GAUSS_SCALE
    return jnp.where(jnp.abs(offset) <= REACH, value, 0.0)


def split(value):
    high = value.astype(BF16)
    return high, (value - high.astype(F32)).astype(BF16)


def dot(a, b):
    return jnp.dot(a, b, preferred_element_type=F32)


def dot_exact(a, b):
    high, low = split(a)
    b = b.astype(BF16)
    return dot(high, b) + dot(low, b)


def exact_dot(a, b):
    high, low = split(b)
    a = a.astype(BF16)
    return dot(a, high) + dot(a, low)


def dot3(a, b):
    ah, al = split(a)
    bh, bl = split(b)
    return dot(ah, bh) + (dot(al, bh) + dot(ah, bl))


def correct_kernel(
    cov, fogr, fogc, x_out, coarse_out,
    ext, cb, rs, cs, hhi, hlo, tt, asum, qhi, qlo, h2hi, h2lo,
    s1, s2, sps, wcat, b0, b16, row24, mbuf, mext, pbuf, abuf, bext, ebuf, fr, fc,
    load_sem, fog_sem, halo_send, halo_recv,
    m_send, m_recv, a_send, a_recv, p_send, p_recv, e_send, e_recv,
    ms_send, ms_recv, bs_send, bs_recv,
):
    stripe = lax.axis_index("stripe")
    row = lax.axis_index("row")
    col = lax.axis_index("col")
    px = row // SIDE
    py = lax.rem(row, SIDE)
    other = 1 - col
    rows, cols = 256, cov.shape[1]
    cells = cols // BS
    wide = cols + 128
    last = SIDE * SIDE - 1

    loads = []
    for i in range(8):
        copy = pltpu.make_async_copy(
            cov.at[pl.ds(32 * i, 32), :],
            ext.at[pl.ds(16 + 32 * i, 32), pl.ds(128, cols)],
            load_sem.at[i],
        )
        copy.start()
        loads.append(copy)
    fog_loads = [
        pltpu.make_async_copy(fogr, fr, fog_sem.at[0]),
        pltpu.make_async_copy(fogc, fc, fog_sem.at[1]),
    ]
    for copy in fog_loads:
        copy.start()

    ext[0:16, :] = jnp.zeros((16, cols + 256), I32)
    ext[272:288, :] = jnp.zeros((16, cols + 256), I32)
    ext[16:272, 0:128] = jnp.zeros((256, 128), I32)
    ext[16:272, cols + 128 : cols + 256] = jnp.zeros((256, 128), I32)
    for buf in (mext, bext):
        buf[0:48, :] = jnp.zeros((48, 128), F32)
        buf[112:160, :] = jnp.zeros((48, 128), F32)

    def at(x, y, c):
        return (stripe, x * SIDE + y, c)

    barrier = pltpu.get_barrier_semaphore()

    def greet(target):
        pl.semaphore_signal(barrier, inc=1, device_id=target, device_id_type=MESH)

    for d in ORDER:
        for c in (0, 1):
            greet(at(px, lax.rem(py + d, SIDE), c))
        greet(at(lax.rem(px + d, SIDE), py, col))
    greet(at(px, py, other))
    crosses_up = jnp.logical_and(py == 0, px > 0)
    crosses_down = jnp.logical_and(py == SIDE - 1, px < SIDE - 1)

    @pl.when(crosses_up)
    def _():
        for c in (0, 1):
            greet((stripe, row - 1, c))

    @pl.when(crosses_down)
    def _():
        for c in (0, 1):
            greet((stripe, row + 1, c))

    for i in range(cols // 256):
        part = (iota((256, 128), 0) + 256 * i) // BS + cells * col
        s1[256 * i : 256 * i + 256, :] = onehot(part == iota((256, 128), 1)).astype(BF16)
    wh, wl = split(taps_of(iota((256, 128), 0) - iota((256, 128), 1) - 64))
    wcat[:, 0:128] = wh
    wcat[:, 128:256] = wl

    for i in range(8):
        loads[i].wait()
        x = ext[16 + 32 * i : 48 + 32 * i, 128 : cols + 128].astype(F32)
        rs[8 * i : 8 * i + 8, :] = x.reshape(4, 8, cols).sum(axis=0)
        cb[16 + 32 * i : 48 + 32 * i, 128 : cols + 128] = x.astype(BF16)
    sums = dot_exact(rs[...], s1[...])
    means = sums.reshape(8, 8, 128).sum(axis=1) * (1.0 / (255.0 * BS * BS))
    mbuf[col, py] = means

    pl.semaphore_wait(
        barrier,
        22 + 2 * crosses_up.astype(I32) + 2 * crosses_down.astype(I32),
    )

    pending = []

    def send(src, dst, s_sem, r_sem, target):
        copy = pltpu.make_async_remote_copy(
            src_ref=src, dst_ref=dst, send_sem=s_sem, recv_sem=r_sem,
            device_id=target, device_id_type=MESH,
        )
        copy.start()
        pending.append((None, copy))

    def send_if(condition, src, dst, s_sem, r_sem, target):
        copy = pltpu.make_async_remote_copy(
            src_ref=src, dst_ref=dst, send_sem=s_sem, recv_sem=r_sem,
            device_id=target, device_id_type=MESH,
        )

        @pl.when(condition)
        def _():
            copy.start()

        pending.append((condition, copy))

    def arrived(dst, r_sem, s_sem):
        pltpu.make_async_remote_copy(
            src_ref=dst, dst_ref=dst, send_sem=s_sem, recv_sem=r_sem,
            device_id=at(px, py, other), device_id_type=MESH,
        ).wait_recv()

    def spread_y(buf, s_sem, r_sem):
        mine = buf.at[col, py]
        slot = r_sem.at[col * SIDE + py]
        for n, d in enumerate(ORDER):
            for c in (0, 1):
                send(mine, mine, s_sem.at[2 * n + c], slot, at(px, lax.rem(py + d, SIDE), c))
        send(mine, mine, s_sem.at[14], slot, at(px, py, other))

    def collect_y(buf, s_sem, r_sem):
        for d in ORDER:
            for c in (0, 1):
                y = lax.rem(py + d, SIDE)
                arrived(buf.at[c, y], r_sem.at[c * SIDE + y], s_sem.at[0])
        arrived(buf.at[other, py], r_sem.at[other * SIDE + py], s_sem.at[0])
        return (buf[0] + buf[1]).reshape(64, 128)

    def spread_x(buf, s_sem, r_sem):
        for n, d in enumerate(ORDER):
            send(buf.at[px], buf.at[px], s_sem.at[n], r_sem.at[px], at(lax.rem(px + d, SIDE), py, col))

    def collect_x(buf, s_sem, r_sem):
        for d in ORDER:
            x = lax.rem(px + d, SIDE)
            arrived(buf.at[x], r_sem.at[x], s_sem.at[0])

    def spread_slabs(buf, s_sem, r_sem):
        send_if(px < SIDE - 1, buf.at[pl.ds(64, 48), :], buf.at[pl.ds(0, 48), :],
                s_sem.at[0], r_sem.at[0], at(px + 1, py, col))
        send_if(px > 0, buf.at[pl.ds(48, 48), :], buf.at[pl.ds(112, 48), :],
                s_sem.at[1], r_sem.at[1], at(px - 1, py, col))

    def collect_slabs(buf, s_sem, r_sem):
        @pl.when(px > 0)
        def _():
            arrived(buf.at[pl.ds(0, 48), :], r_sem.at[0], s_sem.at[0])

        @pl.when(px < SIDE - 1)
        def _():
            arrived(buf.at[pl.ds(112, 48), :], r_sem.at[1], s_sem.at[1])

    spread_y(mbuf, m_send, m_recv)
    own = pl.ds(128, cols)
    inner = pl.ds(pl.multiple_of((1 - col) * (cols - 128) + 128, 128), 128)
    pad_there = pl.ds(pl.multiple_of(col * (cols + 128), 128), 128)
    pad_here = pl.ds(pl.multiple_of(other * (cols + 128), 128), 128)
    body, top, bottom = pl.ds(16, 256), pl.ds(8, 8), pl.ds(272, 8)
    send(ext.at[body, inner], ext.at[body, pad_there], halo_send.at[0], halo_recv.at[0], at(px, py, other))
    up, down = row > 0, row < last
    first8, last8 = pl.ds(16, 8), pl.ds(264, 8)
    send_if(up, ext.at[first8, own], ext.at[bottom, own], halo_send.at[1], halo_recv.at[1], (stripe, row - 1, col))
    send_if(down, ext.at[last8, own], ext.at[top, own], halo_send.at[2], halo_recv.at[2], (stripe, row + 1, col))
    send_if(up, ext.at[first8, inner], ext.at[bottom, pad_there], halo_send.at[3], halo_recv.at[3], (stripe, row - 1, other))
    send_if(down, ext.at[last8, inner], ext.at[top, pad_there], halo_send.at[4], halo_recv.at[4], (stripe, row + 1, other))

    for i in range(wide // 128):
        part = (iota((128, 128), 0) + 128 * i - 64) // BS
        lanes = iota((128, 128), 1)
        inside = jnp.logical_and(part >= 0, part < cells)
        s2[128 * i : 128 * i + 128, :] = onehot(
            jnp.logical_and(inside, part + cells * col == lanes)
        ).astype(BF16)
        cell = (iota((128, 128), 1) + 128 * i + cols * col - 64 + 128) // BS - 4
        sps[:, 128 * i : 128 * i + 128] = onehot(cell == iota((128, 128), 0)).astype(BF16)
    bh, bl = split(taps_of(iota((144, 160), 1) - iota((144, 160), 0)))
    b0[0:144, :] = bh
    b0[144:288, :] = bl
    bh, bl = split(taps_of(iota((144, 160), 1) - iota((144, 160), 0) - 16))
    b16[0:144, :] = bh
    b16[144:288, :] = bl

    def blur_across(src_hi, src_lo, dst_hi, dst_lo, first, count, tiles):
        for j in range(tiles):
            wide_part = dot(src_hi[first : first + count, 128 * j : 128 * j + 256], wcat[...])
            part = wide_part[:, 0:128] + wide_part[:, 128:256]
            if src_lo is not None:
                part = part + dot(src_lo[first : first + count, 128 * j : 128 * j + 256], wcat[:, 0:128])
            high, low = split(part)
            dst_hi[first : first + count, 128 * j : 128 * j + 128] = high
            dst_lo[first : first + count, 128 * j : 128 * j + 128] = low

    arrived(ext.at[body, pad_here], halo_recv.at[0], halo_send.at[0])
    for pad in (0, cols + 128):
        cb[16:272, pad : pad + 128] = ext[16:272, pad : pad + 128].astype(F32).astype(BF16)
    blur_across(cb, None, hhi, hlo, 16, 256, wide // 128)

    mx = collect_y(mbuf, m_send, m_recv)
    mext[48:112, :] = mx
    to_region = jnp.where(
        iota((128, 128), 0) // 8 == lax.rem(iota((128, 128), 1), 16), 1.0 / 64.0, 0.0
    ).astype(BF16)
    own_lanes = iota((64, 128), 1) // 16 == iota((64, 128), 0) // 8

    def region_row(field):
        return jnp.where(own_lanes, dot_exact(field, to_region), 0.0).sum(axis=0, keepdims=True)

    pbuf[px] = region_row(mx)
    spread_slabs(mext, ms_send, ms_recv)
    spread_x(pbuf, p_send, p_recv)

    @pl.when(up)
    def _():
        arrived(ext.at[top, own], halo_recv.at[2], halo_send.at[2])
        arrived(ext.at[top, pad_here], halo_recv.at[4], halo_send.at[4])

    @pl.when(down)
    def _():
        arrived(ext.at[bottom, own], halo_recv.at[1], halo_send.at[1])
        arrived(ext.at[bottom, pad_here], halo_recv.at[3], halo_send.at[3])

    for first in (0, 272):
        cb[first : first + 16, :] = ext[first : first + 16, :].astype(F32).astype(BF16)
        blur_across(cb, None, hhi, hlo, first, 16, wide // 128)

    half = iota((288, 128), 1) < 64
    turned = pltpu.roll(ext[:, 0:128].astype(F32), 64, 1)
    for j in range(wide // 128):
        following = pltpu.roll(ext[:, 128 * j + 128 : 128 * j + 256].astype(F32), 64, 1)
        cs[:, 128 * j : 128 * j + 128] = jnp.where(half, turned, following)
        turned = following

    def blur_down(taps, count, high, low, block, lanes):
        up_part = dot(taps[...] if count == 144 else jnp.concatenate([taps[0:128, :], taps[144:272, :]], 0),
                      high[128 * block : 128 * block + 160, lanes])
        return up_part[0:count] + up_part[count:] + dot(taps[0:count, :], low[128 * block : 128 * block + 160, lanes])

    tiles = [slice(256 * j, 256 * j + 256) for j in range(wide // 256)]
    if wide % 256:
        tiles.append(slice(wide - 128, wide))
    for lanes in tiles:
        for block, taps in ((0, b0), (1, b16)):
            t = 1.5 - blur_down(taps, 144, hhi, hlo, block, lanes) * (0.5 / 255.0)
            tt[144 * block : 144 * block + 144, lanes] = t
            kept = slice(16, 144) if block == 0 else slice(0, 128)
            product = cs[16 + 128 * block : 144 + 128 * block, lanes] * t[kept]
            width = lanes.stop - lanes.start
            asum[32 * block : 32 * block + 32, lanes] = (
                product.reshape(4, 4, 8, width).sum(axis=1).reshape(32, width)
            )
    sums = dot_exact(asum[...], s2[...])
    abuf[col, py] = sums.reshape(8, 8, 128).sum(axis=1) * (1.0 / (255.0 * BS * BS))
    spread_y(abuf, a_send, a_recv)

    across = gauss_of(iota((128, 128), 0) - iota((128, 128), 1))
    across = jnp.where(
        jnp.logical_and(iota((128, 128), 0) < 2 * cells, iota((128, 128), 1) < 2 * cells), across, 0.0
    )
    ah, al = split(across)

    def dot_across(field):
        fh, fl = split(field)
        return dot(fh, ah) + (dot(fl, ah) + dot(fh, al))

    collect_slabs(mext, ms_send, ms_recv)
    swept = dot_across(mext[...])
    back_x = dot3(gauss_of(iota((64, 160), 0) - iota((64, 160), 1) + 48), swept)
    back_24 = dot3(gauss_of(iota((24, 160), 0) - iota((24, 160), 1) + 40 + 8 * py), swept)

    ax = collect_y(abuf, a_send, a_recv)
    bx = ax - 0.3 * back_x * mext[48:112, :]
    bext[48:112, :] = bx
    ebuf[px] = region_row(bx)
    spread_x(ebuf, e_send, e_recv)
    spread_slabs(bext, bs_send, bs_recv)

    for copy in fog_loads:
        copy.wait()
    kr = fr[...]
    kr = kr / jnp.sum(kr, axis=1, keepdims=True)
    kc = fc[...]
    kc = kc / jnp.sum(kc, axis=1, keepdims=True)
    nreg = 2 * cells // 8
    pick = onehot(lax.rem(iota((128, nreg), 0), 16) == iota((128, nreg), 1))
    kct = kc.T
    to_cells = dot_exact(kct, onehot(iota((nreg, 128), 1) // 8 == iota((nreg, 128), 0)))
    to_lanes = dot_exact(kct, onehot(lax.rem(iota((nreg, 128), 1), 16) == iota((nreg, 128), 0)))
    zc = exact_dot(pick, to_cells)
    zl = exact_dot(pick, to_lanes)
    own_kr = jnp.where(iota((64, 64), 0) == row, kr, 0.0).sum(axis=0, keepdims=True)
    own_kr = jnp.where(iota((8, 64), 1) // 8 == iota((8, 64), 0), own_kr, 0.0)
    own_kr = dot_exact(own_kr, onehot(lax.rem(iota((64, 128), 0), 8) == iota((64, 128), 1) // 16))
    collect_x(pbuf, p_send, p_recv)
    regions = pbuf[...]
    spread = jnp.broadcast_to(regions, (8, 8, 128)).reshape(64, 128)
    in_block = iota((64, 128), 1) // 16 == lax.rem(iota((64, 128), 0), 8)
    spread = jnp.where(in_block, spread, 0.0)
    fog_cells = dot3(kr, dot3(spread, zc))
    fog_lanes = dot3(kr, dot3(spread, zl))
    fog_lanes = jnp.where(in_block, fog_lanes, 0.0).reshape(8, 8, 128).sum(axis=1)
    fog_24 = exact_dot(onehot(row - 1 + iota((24, 64), 0) // 8 == iota((24, 64), 1)), fog_cells)
    fog_160 = exact_dot(onehot(8 * px - 6 + iota((160, 64), 0) // 8 == iota((160, 64), 1)), fog_cells)

    coarse = 0.3 * back_24 + 0.2 * fog_24
    row24[...] = dot_exact(coarse, sps[...])
    for first, count, place in [(0, 16, 7)] + [(16 + 32 * i, 32, 8 + i) for i in range(8)] + [(272, 16, 16)]:
        here = slice(first, first + count)
        dose = tt[here, :] - row24[place : place + 1, :]
        tt[here, :] = dose
        high, low = split(cs[here, :] * dose)
        qhi[here, :] = high
        qlo[here, :] = low
    blur_across(qhi, qlo, h2hi, h2lo, 0, 288, cols // 128)
    left = iota((128, 128), 1) < 64
    for j in range(cols // 256):
        lanes = slice(256 * j, 256 * j + 256)
        for block in (0, 1):
            fine = blur_down(b16, 128, h2hi, h2lo, block, lanes)
            here = slice(16 + 128 * block, 144 + 128 * block)
            turned = [pltpu.roll(tt[here, 256 * j + 128 * i : 256 * j + 128 * i + 128], 64, 1) for i in range(3)]
            for i in (0, 1):
                dose = jnp.where(left, turned[i], turned[i + 1])
                x_out[128 * block : 128 * block + 128, 256 * j + 128 * i : 256 * j + 128 * i + 128] = (
                    dose + 0.5 - fine[:, 128 * i : 128 * i + 128] * (0.5 / 255.0)
                )

    collect_slabs(bext, bs_send, bs_recv)
    means2 = bext[...] - 0.2 * fog_160 * mext[...]
    back2 = dot3(gauss_of(iota((8, 160), 0) - iota((8, 160), 1) + 48 + 8 * py), dot_across(means2))
    collect_x(ebuf, e_send, e_recv)
    fog_mean2 = ebuf[...].reshape(8, 128) - 0.2 * fog_lanes * regions.reshape(8, 128)
    weighted = jnp.broadcast_to((own_kr * fog_mean2).sum(axis=0, keepdims=True), (8, 128))
    coarse2 = 0.3 * back2 + 0.2 * dot3(weighted, zc)
    coarse_out[...] = dot_exact(coarse2, sps[:, 64 : cols + 64])

    for condition, copy in pending:
        if condition is None:
            copy.wait_send()
        else:
            pl.when(condition)(copy.wait_send)


def finish_kernel(x, coarse, out, buf, sem):
    cols = coarse.shape[1]
    copies = []
    for i in range(8):
        here = pl.ds(32 * i, 32)
        buf[32 * i : 32 * i + 32, :] = x[32 * i : 32 * i + 32, :] - coarse[i : i + 1, :]
        copy = pltpu.make_async_copy(buf.at[here, :], out.at[here, :], sem.at[i])
        copy.start()
        copies.append(copy)
    for copy in copies:
        copy.wait()


def shards(coverage, fog_rows, fog_cols):
    rows, cols = coverage.shape
    wide = cols + 128
    dma = pltpu.SemaphoreType.DMA
    hbm = pl.BlockSpec(memory_space=pl.ANY)
    vmem = pl.BlockSpec(memory_space=pltpu.VMEM)
    x, coarse = pl.pallas_call(
        correct_kernel,
        out_shape=(
            jax.ShapeDtypeStruct((rows, cols), F32),
            jax.ShapeDtypeStruct((8, cols), F32),
        ),
        in_specs=[hbm, hbm, hbm],
        out_specs=(vmem, vmem),
        scratch_shapes=[
            pltpu.VMEM((288, cols + 256), I32),
            pltpu.VMEM((288, cols + 256), BF16),
            pltpu.VMEM((64, cols), F32),
            pltpu.VMEM((288, wide), F32),
            pltpu.VMEM((288, wide), BF16),
            pltpu.VMEM((288, wide), BF16),
            pltpu.VMEM((288, wide), F32),
            pltpu.VMEM((64, wide), F32),
            pltpu.VMEM((288, wide), BF16),
            pltpu.VMEM((288, wide), BF16),
            pltpu.VMEM((288, cols), BF16),
            pltpu.VMEM((288, cols), BF16),
            pltpu.VMEM((cols, 128), BF16),
            pltpu.VMEM((wide, 128), BF16),
            pltpu.VMEM((128, wide), BF16),
            pltpu.VMEM((256, 256), BF16),
            pltpu.VMEM((288, 160), BF16),
            pltpu.VMEM((288, 160), BF16),
            pltpu.VMEM((24, wide), F32),
            pltpu.VMEM((2, SIDE, 8, 128), F32),
            pltpu.VMEM((160, 128), F32),
            pltpu.VMEM((SIDE, 1, 128), F32),
            pltpu.VMEM((2, SIDE, 8, 128), F32),
            pltpu.VMEM((160, 128), F32),
            pltpu.VMEM((SIDE, 1, 128), F32),
            pltpu.VMEM(fog_rows.shape, F32),
            pltpu.VMEM(fog_cols.shape, F32),
            dma((8,)), dma((2,)), dma((5,)), dma((5,)),
            dma((16,)), dma((16,)), dma((16,)), dma((16,)),
            dma((8,)), dma((8,)), dma((8,)), dma((8,)),
            dma((2,)), dma((2,)), dma((2,)), dma((2,)),
        ],
        compiler_params=pltpu.CompilerParams(
            collective_id=0, has_side_effects=True, vmem_limit_bytes=44 * 1024 * 1024
        ),
    )(coverage, fog_rows, fog_cols)
    return pl.pallas_call(
        finish_kernel,
        out_shape=jax.ShapeDtypeStruct((rows, cols), F32),
        in_specs=[vmem, vmem],
        out_specs=hbm,
        scratch_shapes=[pltpu.VMEM((rows, cols), F32), dma((8,))],
        compiler_params=pltpu.CompilerParams(vmem_limit_bytes=8 * 1024 * 1024),
    )(x, coarse)


def solution(mesh):
    placed = (P(("stripe", "row"), "col"), P(), P())
    return jax.shard_map(
        shards, mesh=mesh, in_specs=placed, out_specs=P(("stripe", "row"), "col"), check_vma=False
    )
```

time: 185 us -> 45 us (0.24)
  other arithmetic: 60 us -> 0 us
  starting transfers between devices: 57.2 us -> 0 us
  local copies, waits for them, and re-layouts: 52.5 us -> 3.04 us
  Pallas kernels: 0 us -> 41.7 us
  blocking collectives: 8.87 us -> 0 us
  matrix products: 3.4 us -> 0 us
    pallas_call x0 -> x2, Pallas kernels: none -> 41.7 us  [the longest x1 40.3 us: shards(): pl.pallas_call(correct_kernel, out_shape=(jax.ShapeDtypeStruct((rows, col...]
    all_to_all x2 -> x0, starting transfers between devices: 36.8 us -> none  [from_everyone(): lax.all_to_all(jnp.broadcast_to(value[None], (count, *value.shape)), axis...]
    add x5 -> x0, other arithmetic: 30 us -> none  [the longest x2 17.5 us: blur_padded(): across = across + taps[index] * padded[index:index + rows, :]]
    add x4 -> x0, local copies, waits for them, and re-layouts: 24.1 us -> none  [spread_add(): field.reshape(rows // size, size, cols // size, size)]
    ppermute x8 -> x0, starting transfers between devices: 20.4 us -> none  [the longest x4 10.9 us: extended(): before = lax.ppermute(last, axis, up)]
    mul x1 -> x0, other arithmetic: 12.5 us -> none  [shards(): charge = dose * cover]
    reshape x4 -> x0, local copies, waits for them, and re-layouts: 11.7 us -> none  [the longest x2 11.1 us: block_mean(): field.reshape(rows // size, size, cols // size, size).sum(axis=(1, 3))]
    reduce_sum x9 -> x0, other arithmetic: 9.78 us -> none  [the longest x6 8.86 us: block_mean(): field.reshape(rows // size, size, cols // size, size).sum(axis=(1, 3))]
  transfers between devices with their start and end apart: 10 -> 0, of which waited for: 1 -> 0; matrix products, arithmetic and copies ran while one was open for 26% -> 0% of each run, Pallas kernels for 0% -> 0%
where the time goes in v1:
time: 45 us; the launch traced here: 44.8 us
  Pallas kernels  41.7 us (93%)
  local copies, waits for them, and re-layouts  3.04 us (7%)
    pallas_call x1, Pallas kernels, shards(): pl.pallas_call(correct_kernel, out_shape=(jax.ShapeDtypeStruct((rows, col...  40.3 us
    unnamed x6, local copies, waits for them, and re-layouts  3.04 us
    pallas_call x1, Pallas kernels, shards(): pl.pallas_call(finish_kernel, out_shape=jax.ShapeDtypeStruct((rows, cols)...  1.4 us

profile of v1, /device:TPU:513, one launch (start us, length us, event | category | flops | bytes accessed | tf_op | source)
XLA Modules:
  0.0 44.8 jit_solution(2583509457095207604)
XLA Ops:
  0.0 0.0 copy-start
  0.0 1.6 %copy-done = s32[256,2048]{1,0:T(8,128)S(1)} copy-done((s32[256,2048]{1,0:T(8,128)S(1)}, s32[256,2048]{1,0:T(8,128)}, u32[]{:S(2)}) %copy-start) | copy-done | bytes 2097176
  1.6 0.0 copy-start.1
  1.6 0.8 %copy-done.1 = f32[64,64]{1,0:T(8,128)S(1)} copy-done((f32[64,64]{1,0:T(8,128)S(1)}, f32[64,64]{1,0:T(8,128)}, u32[]{:S(2)}) %copy-start.1) | copy-done | bytes 16408
  2.4 0.0 copy-start.2
  2.4 0.7 %copy-done.2 = f32[16,16]{1,0:T(8,128)S(1)} copy-done((f32[16,16]{1,0:T(8,128)S(1)}, f32[16,16]{1,0:T(8,128)}, u32[]{:S(2)}) %copy-start.2) | copy-done | bytes 1048
  3.0 40.3 %shard_map.37 = (f32[256,2048]{1,0:T(8,128)S(1)}, f32[8,2048]{1,0:T(8,128)S(1)}) custom-call(s32[256,2048]{1,0:T(8,128)S(1)} %copy-done, f32[64,64]{1,0:T(8,128)S(1)} %copy-done.1, f32[16,16]{1,0:T(8,128)S(1)} %copy-done.2), custom_call_target="tpu_custom_call" | custom-call | tf_op jit(solution)/shard_map/pallas_call | solution.py:441
  43.4 1.4 %shard_map.38 = f32[256,2048]{1,0:T(8,128)} custom-call(f32[256,2048]{1,0:T(8,128)S(1)} %get-tuple-element.7.x, f32[8,2048]{1,0:T(8,128)S(1)} %get-tuple-element.8.coarse), custom_call_target="tpu_custom_call" | custom-call | tf_op jit(solution)/shard_map/pallas_call | solution.py:486
Async XLA Ops:
  0.0 1.6 %copy-start = (s32[256,2048]{1,0:T(8,128)S(1)}, s32[256,2048]{1,0:T(8,128)}, u32[]{:S(2)}) copy-start(s32[256,2048]{1,0:T(8,128)} %cov.1) | copy-start | bytes 6291460
  1.6 0.8 %copy-start.1 = (f32[64,64]{1,0:T(8,128)S(1)}, f32[64,64]{1,0:T(8,128)}, u32[]{:S(2)}) copy-start(f32[64,64]{1,0:T(8,128)} %fogr.1) | copy-start | bytes 49156
  2.4 0.7 %copy-start.2 = (f32[16,16]{1,0:T(8,128)S(1)}, f32[16,16]{1,0:T(8,128)}, u32[]{:S(2)}) copy-start(f32[16,16]{1,0:T(8,128)} %fogc.1) | copy-start | bytes 3076

commit v2 on v1

v2 whole, which is shorter than its diff:
```python
import math

import jax
import jax.numpy as jnp
from jax import lax
from jax.experimental import pallas as pl
from jax.experimental.pallas import tpu as pltpu
from jax.sharding import PartitionSpec as P

BS = 32
FB = 256
HALO = 4
BSIG = 16
REACH = 40
SIDE = 8
MESH = pl.DeviceIdType.MESH
F32 = jnp.float32
BF16 = jnp.bfloat16
I32 = jnp.int32
ORDER = (4, 3, 5, 2, 6, 1, 7)

TAPS = [math.exp(-(k * k) / (2 * 1.25**2)) for k in range(-HALO, HALO + 1)]
TAP_SCALE = 1.0 / sum(TAPS)
GAUSS_SCALE = 1.0 / (BSIG * math.sqrt(2.0 * math.pi))


def iota(shape, dim):
    return lax.broadcasted_iota(I32, shape, dim)


def onehot(condition):
    return jnp.where(condition, 1.0, 0.0).astype(F32)


def taps_of(offset):
    square = (offset * offset).astype(F32)
    value = jnp.exp(square * (-1.0 / (2 * 1.25**2))) * TAP_SCALE
    return jnp.where(jnp.abs(offset) <= HALO, value, 0.0)


def gauss_of(offset):
    square = (offset * offset).astype(F32)
    value = jnp.exp(square * (-0.5 / (BSIG * BSIG))) * GAUSS_SCALE
    return jnp.where(jnp.abs(offset) <= REACH, value, 0.0)


def split(value):
    high = value.astype(BF16)
    return high, (value - high.astype(F32)).astype(BF16)


def dot(a, b):
    return jnp.dot(a, b, preferred_element_type=F32)


def dot_exact(a, b):
    high, low = split(a)
    b = b.astype(BF16)
    return dot(high, b) + dot(low, b)


def exact_dot(a, b):
    high, low = split(b)
    a = a.astype(BF16)
    return dot(a, high) + dot(a, low)


def dot3(a, b):
    ah, al = split(a)
    bh, bl = split(b)
    return dot(ah, bh) + (dot(al, bh) + dot(ah, bl))


def correct_kernel(
    cov, fogr, fogc, x_out, coarse_out,
    ext, cb, rs, cs, hhi, hlo, tt, asum, qhi, qlo, h2hi, h2lo,
    s1, s2, sps, wcat, b16, zp, row24, mbuf, mext, pbuf, abuf, bext, ebuf, fr, fc,
    edge_sem, load_sem, fog_sem, halo_send, halo_recv, ready,
    m_sem, a_sem, p_sem, e_sem, ms_sem, bs_sem,
):
    stripe = lax.axis_index("stripe")
    row = lax.axis_index("row")
    col = lax.axis_index("col")
    px = row // SIDE
    py = lax.rem(row, SIDE)
    other = 1 - col
    rows, cols = 256, cov.shape[1]
    cells = cols // BS
    wide = cols + 128
    last = SIDE * SIDE - 1
    mine = col * SIDE + py

    own = pl.ds(128, cols)
    first8, last8 = pl.ds(16, 8), pl.ds(264, 8)
    for at_row in (0, 248):
        pltpu.make_async_copy(
            cov.at[pl.ds(at_row, 8), :], ext.at[pl.ds(16 + at_row, 8), own], edge_sem
        ).start()
    spans = [(8, 32), (32, 64), (64, 96), (96, 128), (128, 160), (160, 192), (192, 224), (224, 248)]
    for i, (start, stop) in enumerate(spans):
        pltpu.make_async_copy(
            cov.at[pl.ds(start, stop - start), :],
            ext.at[pl.ds(16 + start, stop - start), own],
            load_sem.at[i // 2],
        ).start()
    fog_loads = [
        pltpu.make_async_copy(fogr, fr, fog_sem.at[0]),
        pltpu.make_async_copy(fogc, fc, fog_sem.at[1]),
    ]
    for copy in fog_loads:
        copy.start()

    def whole(ref, sem):
        pltpu.make_async_copy(ref, ref, sem).wait()

    ext[0:16, :] = jnp.zeros((16, cols + 256), I32)
    ext[272:288, :] = jnp.zeros((16, cols + 256), I32)
    ext[16:272, 0:128] = jnp.zeros((256, 128), I32)
    ext[16:272, cols + 128 : cols + 256] = jnp.zeros((256, 128), I32)
    for buf in (mext, bext):
        buf[0:48, :] = jnp.zeros((48, 128), F32)
        buf[112:160, :] = jnp.zeros((48, 128), F32)

    def at(x, y, c):
        return (stripe, x * SIDE + y, c)

    def beside_y(d):
        return lax.rem(py + d, SIDE)

    def beside_x(d):
        return lax.rem(px + d, SIDE)

    barrier = pltpu.get_barrier_semaphore()

    def signal(sem, target):
        pl.semaphore_signal(sem, inc=1, device_id=target, device_id_type=MESH)

    crosses_up = jnp.logical_and(py == 0, px > 0)
    crosses_down = jnp.logical_and(py == SIDE - 1, px < SIDE - 1)
    for d in (1, 7):
        for c in (0, 1):
            signal(barrier, at(px, beside_y(d), c))
        signal(barrier, at(beside_x(d), py, col))
    signal(barrier, at(px, py, other))

    @pl.when(crosses_up)
    def _():
        for c in (0, 1):
            signal(barrier, (stripe, row - 1, c))

    @pl.when(crosses_down)
    def _():
        for c in (0, 1):
            signal(barrier, (stripe, row + 1, c))

    def send(src, dst, s_sem, r_sem, target):
        pltpu.make_async_remote_copy(
            src_ref=src, dst_ref=dst, send_sem=s_sem, recv_sem=r_sem,
            device_id=target, device_id_type=MESH,
        ).start()

    inner = pl.ds(pl.multiple_of((1 - col) * (cols - 128) + 128, 128), 128)
    pad_there = pl.ds(pl.multiple_of(col * (cols + 128), 128), 128)
    pad_here = pl.ds(pl.multiple_of(other * (cols + 128), 128), 128)
    body, top, bottom = pl.ds(16, 256), pl.ds(8, 8), pl.ds(272, 8)
    both = pl.ds(0, cols + 128)
    up, down = row > 0, row < last

    whole(ext.at[pl.ds(16, 16), own], edge_sem)
    pl.semaphore_wait(
        barrier,
        7 + 2 * crosses_up.astype(I32) + 2 * crosses_down.astype(I32),
    )

    @pl.when(up)
    def _():
        send(ext.at[first8, own], ext.at[bottom, own], halo_send.at[1], halo_recv.at[1], (stripe, row - 1, col))
        send(ext.at[first8, inner], ext.at[bottom, pad_there], halo_send.at[1], halo_recv.at[1], (stripe, row - 1, other))

    @pl.when(down)
    def _():
        send(ext.at[last8, own], ext.at[top, own], halo_send.at[2], halo_recv.at[2], (stripe, row + 1, col))
        send(ext.at[last8, inner], ext.at[top, pad_there], halo_send.at[2], halo_recv.at[2], (stripe, row + 1, other))

    for d in (1, 7):
        signal(ready.at[0], at(px, beside_y(d), col))
        signal(ready.at[0], at(beside_x(d), py, col))

    for i in range(cols // 256):
        part = (iota((256, 128), 0) + 256 * i) // BS + cells * col
        s1[256 * i : 256 * i + 256, :] = onehot(part == iota((256, 128), 1)).astype(BF16)
    wh, wl = split(taps_of(iota((256, 128), 0) - iota((256, 128), 1) - 64))
    wcat[:, 0:128] = wh
    wcat[:, 128:256] = wl
    bh, bl = split(taps_of(iota((144, 160), 1) - iota((144, 160), 0) - 16))
    b16[0:144, :] = bh
    b16[144:288, :] = bl
    for i in range(wide // 128):
        part = (iota((128, 128), 0) + 128 * i - 64) // BS
        inside = jnp.logical_and(part >= 0, part < cells)
        s2[128 * i : 128 * i + 128, :] = onehot(
            jnp.logical_and(inside, part + cells * col == iota((128, 128), 1))
        ).astype(BF16)

    for i in range(8):
        if i % 2 == 0:
            start = spans[i][0]
            whole(ext.at[pl.ds(16 + start, spans[i + 1][1] - start), own], load_sem.at[i // 2])
        x = ext[16 + 32 * i : 48 + 32 * i, 128 : cols + 128].astype(F32)
        rs[8 * i : 8 * i + 8, :] = x.reshape(4, 8, cols).sum(axis=0)
        cb[16 + 32 * i : 48 + 32 * i, 128 : cols + 128] = x.astype(BF16)
    sums = dot_exact(rs[...], s1[...])
    means = sums.reshape(8, 8, 128).sum(axis=1) * (1.0 / (255.0 * BS * BS))
    mbuf[mine] = means

    send(ext.at[body, inner], ext.at[body, pad_there], halo_send.at[0], halo_recv.at[0], at(px, py, other))

    pl.semaphore_wait(ready.at[0], 4)
    for d in (2, 6):
        signal(ready.at[1], at(px, beside_y(d), col))
        signal(ready.at[1], at(beside_x(d), py, col))

    def spread_y(buf, sem):
        for d in ORDER:
            for c in (0, 1):
                send(buf.at[mine], buf.at[mine], sem.at[0], sem.at[1], at(px, beside_y(d), c))
        send(buf.at[mine], buf.at[mine], sem.at[0], sem.at[1], at(px, py, other))

    def collect_y(buf, sem):
        whole(buf.at[pl.ds(0, 2 * SIDE - 1)], sem.at[1])
        return (buf[0:SIDE] + buf[SIDE:]).reshape(64, 128)

    def spread_x(buf, sem):
        for d in ORDER:
            send(buf.at[px], buf.at[px], sem.at[0], sem.at[1], at(beside_x(d), py, col))

    def collect_x(buf, sem):
        whole(buf.at[pl.ds(0, SIDE - 1)], sem.at[1])

    def spread_slabs(buf, sem):
        @pl.when(px < SIDE - 1)
        def _():
            send(buf.at[pl.ds(64, 48), :], buf.at[pl.ds(0, 48), :],
                 sem.at[0], sem.at[2], at(px + 1, py, col))

        @pl.when(px > 0)
        def _():
            send(buf.at[pl.ds(48, 48), :], buf.at[pl.ds(112, 48), :],
                 sem.at[1], sem.at[3], at(px - 1, py, col))

    def collect_slabs(buf, sem):
        @pl.when(px > 0)
        def _():
            whole(buf.at[pl.ds(0, 48), :], sem.at[2])

        @pl.when(px < SIDE - 1)
        def _():
            whole(buf.at[pl.ds(112, 48), :], sem.at[3])

    def pieces(ref, parts, lanes):
        found = [ref[first : first + count, lanes] for first, count in parts]
        return found[0] if len(found) == 1 else jnp.concatenate(found, axis=0)

    def put(ref, parts, lanes, value):
        at_row = 0
        for first, count in parts:
            ref[first : first + count, lanes] = value[at_row : at_row + count]
            at_row += count

    def blur_across(src_hi, src_lo, dst_hi, dst_lo, parts, tiles):
        for j in range(tiles):
            window, lanes = slice(128 * j, 128 * j + 256), slice(128 * j, 128 * j + 128)
            wide_part = dot(pieces(src_hi, parts, window), wcat[...])
            part = wide_part[:, 0:128] + wide_part[:, 128:256]
            if src_lo is not None:
                part = part + dot(pieces(src_lo, parts, window), wcat[:, 0:128])
            high, low = split(part)
            put(dst_hi, parts, lanes, high)
            put(dst_lo, parts, lanes, low)

    def shift_coverage(parts):
        count = sum(n for _, n in parts)
        half = iota((count, 128), 1) < 64
        turned = pltpu.roll(pieces(ext, parts, slice(0, 128)).astype(F32), 64, 1)
        for j in range(wide // 128):
            following = pieces(ext, parts, slice(128 * j + 128, 128 * j + 256)).astype(F32)
            following = pltpu.roll(following, 64, 1)
            put(cs, parts, slice(128 * j, 128 * j + 128), jnp.where(half, turned, following))
            turned = following

    def blur_down(count, depth, high, low, first, lanes):
        both = jnp.concatenate([b16[0:count, 0:depth], b16[144 : 144 + count, 0:depth]], 0)
        here = slice(first, first + depth)
        result = dot(both, high[here, lanes])
        return result[0:count] + result[count:] + dot(b16[0:count, 0:depth], low[here, lanes])

    body_rows, edge_rows = ((16, 256),), ((0, 16), (272, 16))
    whole(ext.at[body, pad_here], halo_recv.at[0])
    for pad in (0, cols + 128):
        cb[16:272, pad : pad + 128] = ext[16:272, pad : pad + 128].astype(F32).astype(BF16)
    blur_across(cb, None, hhi, hlo, body_rows, wide // 128)
    shift_coverage(body_rows)

    tiles = [slice(256 * j, 256 * j + 256) for j in range(wide // 256)]
    if wide % 256:
        tiles.append(slice(wide - 128, wide))

    def main_rows(lanes):
        width = lanes.stop - lanes.start
        for block in (0, 1):
            here = slice(32 + 112 * block, 144 + 112 * block)
            t = 1.5 - blur_down(112, 144, hhi, hlo, 16 + 112 * block, lanes) * (0.5 / 255.0)
            tt[here, lanes] = t
            product = cs[here, lanes] * t
            whole = product[16:112] if block == 0 else product[0:96]
            half = product[0:16] if block == 0 else product[96:112]
            whole = whole.reshape(3, 4, 8, width).sum(axis=1).reshape(24, width)
            asum[8 + 24 * block : 32 + 24 * block, lanes] = whole
            asum[56 * block : 56 * block + 8, lanes] = half[0:8] + half[8:16]

    for lanes in tiles:
        main_rows(lanes)

    pl.semaphore_wait(ready.at[1], 4)
    spread_y(mbuf, m_sem)

    for i in range(wide // 128):
        cell = (iota((128, 128), 1) + 128 * i + cols * col - 64 + 128) // BS - 4
        sps[:, 128 * i : 128 * i + 128] = onehot(cell == iota((128, 128), 0)).astype(BF16)

    to_region = jnp.where(
        iota((128, 128), 0) // 8 == lax.rem(iota((128, 128), 1), 16), 1.0 / 64.0, 0.0
    ).astype(BF16)
    own_lanes = iota((64, 128), 1) // 16 == iota((64, 128), 0) // 8

    def region_row(field):
        return jnp.where(own_lanes, dot_exact(field, to_region), 0.0).sum(axis=0, keepdims=True)

    across = gauss_of(iota((128, 128), 0) - iota((128, 128), 1))
    across = jnp.where(
        jnp.logical_and(iota((128, 128), 0) < 2 * cells, iota((128, 128), 1) < 2 * cells), across, 0.0
    )
    ah, al = split(across)

    def dot_across(field):
        fh, fl = split(field)
        return dot(fh, ah) + (dot(fl, ah) + dot(fh, al))

    for copy in fog_loads:
        copy.wait()
    kr = fr[...]
    kr = kr / jnp.sum(kr, axis=1, keepdims=True)
    kc = fc[...]
    kc = kc / jnp.sum(kc, axis=1, keepdims=True)
    nreg = 2 * cells // 8
    pick = onehot(lax.rem(iota((128, nreg), 0), 16) == iota((128, nreg), 1))
    kct = kc.T
    to_cells = dot_exact(kct, onehot(iota((nreg, 128), 1) // 8 == iota((nreg, 128), 0)))
    to_lanes = dot_exact(kct, onehot(lax.rem(iota((nreg, 128), 1), 16) == iota((nreg, 128), 0)))
    zc = exact_dot(pick, to_cells)
    zl = exact_dot(pick, to_lanes)
    zboth = jnp.concatenate([zc, zl], axis=1)
    in_block = iota((64, 128), 1) // 16 == lax.rem(iota((64, 128), 0), 8)
    kr_24 = exact_dot(onehot(row - 1 + iota((24, 64), 0) // 8 == iota((24, 64), 1)), kr)
    kr_160 = exact_dot(onehot(8 * px - 6 + iota((160, 64), 0) // 8 == iota((160, 64), 1)), kr)
    own_kr = jnp.where(iota((64, 64), 0) == row, kr, 0.0).sum(axis=0, keepdims=True)
    own_kr = jnp.where(iota((8, 64), 1) // 8 == iota((8, 64), 0), own_kr, 0.0)
    own_kr = dot_exact(own_kr, onehot(lax.rem(iota((64, 128), 0), 8) == iota((64, 128), 1) // 16))
    zph, zpl = split(dot_exact(0.2 * zc, sps[:, 64 : cols + 64]))
    zp[0] = zph
    zp[1] = zpl
    part, side = iota((128, 192), 0) // 64, lax.rem(iota((128, 192), 0) // 32, 2)
    piece = iota((128, 192), 1) // 48
    value = taps_of(lax.rem(iota((128, 192), 1), 48) - lax.rem(iota((128, 192), 0), 32) - 16 * side)
    high, low = split(value)
    value = jnp.where(part == 0, high.astype(F32), jnp.where(lax.rem(piece, 2) == 0, low.astype(F32), 0.0))
    edge_taps = jnp.where(side == piece // 2, value, 0.0).astype(BF16)


    @pl.when(up)
    def _():
        whole(ext.at[top, both], halo_recv.at[2])

    @pl.when(down)
    def _():
        whole(ext.at[bottom, both], halo_recv.at[1])

    for first in (0, 272):
        cb[first : first + 16, :] = ext[first : first + 16, :].astype(F32).astype(BF16)
    blur_across(cb, None, hhi, hlo, edge_rows, wide // 128)
    shift_coverage(edge_rows)
    for lanes in tiles:
        inputs = jnp.concatenate(
            [hhi[0:48, lanes], hlo[0:48, lanes], hhi[240:288, lanes], hlo[240:288, lanes]], 0
        )
        result = dot(edge_taps, inputs)
        t = 1.5 - (result[0:64] + result[64:128]) * (0.5 / 255.0)
        tt[0:32, lanes] = t[0:32]
        tt[256:288, lanes] = t[32:64]
        product = cs[16:32, lanes] * t[16:32]
        asum[64:72, lanes] = product[0:8] + product[8:16]
        product = cs[256:272, lanes] * t[32:48]
        asum[72:80, lanes] = product[0:8] + product[8:16]
    sums = dot_exact(asum[...], s2[...]).reshape(10, 8, 128).sum(axis=1)
    cell_row = iota((8, 128), 0)
    sums = (
        sums[0:8]
        + jnp.where(cell_row == 0, sums[8:9], 0.0)
        + jnp.where(cell_row == 7, sums[9:10], 0.0)
    )
    abuf[mine] = sums * (1.0 / (255.0 * BS * BS))
    spread_y(abuf, a_sem)

    mx = collect_y(mbuf, m_sem)
    mext[48:112, :] = mx
    pbuf[px] = region_row(mx)
    spread_x(pbuf, p_sem)
    spread_slabs(mext, ms_sem)
    collect_slabs(mext, ms_sem)
    swept = dot_across(mext[...])
    back_x = dot3(gauss_of(iota((64, 160), 0) - iota((64, 160), 1) + 48), swept)
    back_24 = dot3(gauss_of(iota((24, 160), 0) - iota((24, 160), 1) + 40 + 8 * py), swept)

    ax = collect_y(abuf, a_sem)
    bx = ax - 0.3 * back_x * mext[48:112, :]
    bext[48:112, :] = bx
    ebuf[px] = region_row(bx)
    spread_x(ebuf, e_sem)
    spread_slabs(bext, bs_sem)

    collect_x(pbuf, p_sem)
    regions = pbuf[...]
    spread = jnp.broadcast_to(regions, (8, 8, 128)).reshape(64, 128)
    fog_wide = dot3(jnp.where(in_block, spread, 0.0), zboth)
    fog_24 = dot3(kr_24, fog_wide[:, 0:128])

    coarse = 0.3 * back_24 + 0.2 * fog_24
    row24[...] = dot_exact(coarse, sps[...])
    fog_lanes = jnp.where(in_block, dot3(kr, fog_wide[:, 128:256]), 0.0).reshape(8, 8, 128).sum(axis=1)
    fog_160 = dot3(kr_160, fog_wide[:, 0:128])
    for first, count, place in [(0, 16, 7)] + [(16 + 32 * i, 32, 8 + i) for i in range(8)] + [(272, 16, 16)]:
        here = slice(first, first + count)
        dose = tt[here, :] - row24[place : place + 1, :]
        tt[here, :] = dose
        high, low = split(cs[here, :] * dose)
        qhi[here, :] = high
        qlo[here, :] = low
    blur_across(qhi, qlo, h2hi, h2lo, ((0, 288),), cols // 128)
    left = iota((128, 128), 1) < 64
    for j in range(cols // 256):
        lanes = slice(256 * j, 256 * j + 256)
        for block in (0, 1):
            fine = blur_down(128, 160, h2hi, h2lo, 128 * block, lanes)
            here = slice(16 + 128 * block, 144 + 128 * block)
            turned = [pltpu.roll(tt[here, 256 * j + 128 * i : 256 * j + 128 * i + 128], 64, 1) for i in range(3)]
            for i in (0, 1):
                dose = jnp.where(left, turned[i], turned[i + 1])
                x_out[128 * block : 128 * block + 128, 256 * j + 128 * i : 256 * j + 128 * i + 128] = (
                    dose + 0.5 - fine[:, 128 * i : 128 * i + 128] * (0.5 / 255.0)
                )

    whole(mbuf.at[pl.ds(0, 2 * SIDE - 1)], m_sem.at[0])
    whole(abuf.at[pl.ds(0, 2 * SIDE - 1)], a_sem.at[0])
    whole(pbuf.at[pl.ds(0, SIDE - 1)], p_sem.at[0])
    whole(ebuf.at[pl.ds(0, SIDE - 1)], e_sem.at[0])
    whole(ext.at[body, pad_here], halo_send.at[0])

    @pl.when(up)
    def _():
        whole(ext.at[top, both], halo_send.at[1])

    @pl.when(down)
    def _():
        whole(ext.at[bottom, both], halo_send.at[2])

    for sem in (ms_sem, bs_sem):
        @pl.when(px < SIDE - 1)
        def _():
            whole(mext.at[pl.ds(0, 48), :], sem.at[0])

        @pl.when(px > 0)
        def _():
            whole(mext.at[pl.ds(112, 48), :], sem.at[1])

    collect_slabs(bext, bs_sem)
    means2 = bext[...] - 0.2 * fog_160 * mext[...]
    back2 = dot3(gauss_of(iota((8, 160), 0) - iota((8, 160), 1) + 48 + 8 * py), dot_across(means2))
    coarse_out[...] = dot_exact(0.3 * back2, sps[:, 64 : cols + 64])
    fog_known = 0.2 * fog_lanes * regions.reshape(8, 128)
    collect_x(ebuf, e_sem)
    fog_mean2 = ebuf[...].reshape(8, 128) - fog_known
    weighted = jnp.broadcast_to((own_kr * fog_mean2).sum(axis=0, keepdims=True), (8, 128))
    high, low = split(weighted)
    fog2 = dot(high, zp[0]) + (dot(low, zp[0]) + dot(high, zp[1]))
    coarse_out[...] = coarse_out[...] + fog2


def finish_kernel(x, coarse, out, buf, sem):
    cols = coarse.shape[1]
    copies = []
    for i in range(8):
        here = pl.ds(32 * i, 32)
        buf[32 * i : 32 * i + 32, :] = x[32 * i : 32 * i + 32, :] - coarse[i : i + 1, :]
        copy = pltpu.make_async_copy(buf.at[here, :], out.at[here, :], sem.at[i])
        copy.start()
        copies.append(copy)
    for copy in copies:
        copy.wait()


def shards(coverage, fog_rows, fog_cols):
    rows, cols = coverage.shape
    wide = cols + 128
    dma = pltpu.SemaphoreType.DMA
    hbm = pl.BlockSpec(memory_space=pl.ANY)
    vmem = pl.BlockSpec(memory_space=pltpu.VMEM)
    x, coarse = pl.pallas_call(
        correct_kernel,
        out_shape=(
            jax.ShapeDtypeStruct((rows, cols), F32),
            jax.ShapeDtypeStruct((8, cols), F32),
        ),
        in_specs=[pl.BlockSpec(memory_space=pltpu.MemorySpace.HBM)] * 3,
        out_specs=(vmem, vmem),
        scratch_shapes=[
            pltpu.VMEM((288, cols + 256), I32),
            pltpu.VMEM((288, cols + 256), BF16),
            pltpu.VMEM((64, cols), F32),
            pltpu.VMEM((288, wide), F32),
            pltpu.VMEM((288, wide), BF16),
            pltpu.VMEM((288, wide), BF16),
            pltpu.VMEM((288, wide), F32),
            pltpu.VMEM((80, wide), F32),
            pltpu.VMEM((288, wide), BF16),
            pltpu.VMEM((288, wide), BF16),
            pltpu.VMEM((288, cols), BF16),
            pltpu.VMEM((288, cols), BF16),
            pltpu.VMEM((cols, 128), BF16),
            pltpu.VMEM((wide, 128), BF16),
            pltpu.VMEM((128, wide), BF16),
            pltpu.VMEM((256, 256), BF16),
            pltpu.VMEM((288, 160), BF16),
            pltpu.VMEM((2, 128, cols), BF16),
            pltpu.VMEM((24, wide), F32),
            pltpu.VMEM((2 * SIDE, 8, 128), F32),
            pltpu.VMEM((160, 128), F32),
            pltpu.VMEM((SIDE, 1, 128), F32),
            pltpu.VMEM((2 * SIDE, 8, 128), F32),
            pltpu.VMEM((160, 128), F32),
            pltpu.VMEM((SIDE, 1, 128), F32),
            pltpu.VMEM(fog_rows.shape, F32),
            pltpu.VMEM(fog_cols.shape, F32),
            dma(()), dma((4,)), dma((2,)), dma((3,)), dma((3,)), pltpu.SemaphoreType.REGULAR((2,)),
            dma((2,)), dma((2,)), dma((2,)), dma((2,)), dma((4,)), dma((4,)),
        ],
        compiler_params=pltpu.CompilerParams(
            collective_id=0, has_side_effects=True, vmem_limit_bytes=44 * 1024 * 1024
        ),
    )(*[pltpu.with_memory_space_constraint(v, pltpu.MemorySpace.HBM) for v in (coverage, fog_rows, fog_cols)])
    return pl.pallas_call(
        finish_kernel,
        out_shape=jax.ShapeDtypeStruct((rows, cols), F32),
        in_specs=[vmem, vmem],
        out_specs=hbm,
        scratch_shapes=[pltpu.VMEM((rows, cols), F32), dma((8,))],
        compiler_params=pltpu.CompilerParams(vmem_limit_bytes=8 * 1024 * 1024),
    )(x, coarse)


def solution(mesh):
    placed = (P(("stripe", "row"), "col"), P(), P())
    return jax.shard_map(
        shards, mesh=mesh, in_specs=placed, out_specs=P(("stripe", "row"), "col"), check_vma=False
    )
```

time: 45 us -> 38 us (0.84)
  Pallas kernels: 41.7 us -> 37.9 us
  local copies, waits for them, and re-layouts: 3.04 us -> 0 us
    pallas_call x1, Pallas kernels: 40.3 us -> 36.5 us  [shards(): pl.pallas_call(correct_kernel, out_shape=(jax.ShapeDtypeStruct((rows, col...]
    unnamed x6 -> x0, local copies, waits for them, and re-layouts: 3.04 us -> none
where the time goes in v2:
time: 38 us; the launch traced here: 37.9 us
  Pallas kernels  37.9 us (100%)
    pallas_call x1, Pallas kernels, shards(): pl.pallas_call(correct_kernel, out_shape=(jax.ShapeDtypeStruct((rows, col...  36.5 us
    pallas_call x1, Pallas kernels, shards(): pl.pallas_call(finish_kernel, out_shape=jax.ShapeDtypeStruct((rows, cols)...  1.4 us

profile of v2, /device:TPU:513, one launch (start us, length us, event | category | flops | bytes accessed | tf_op | source)
XLA Modules:
  0.0 37.9 jit_solution(6699722845995439942)
XLA Ops:
  0.0 36.5 %shard_map.37 = (f32[256,2048]{1,0:T(8,128)S(1)}, f32[8,2048]{1,0:T(8,128)S(1)}) custom-call(s32[256,2048]{1,0:T(8,128)} %cov.1, f32[64,64]{1,0:T(8,128)} %fogr.1, f32[16,16]{1,0:T(8,128)} %fogc.1), custom_call_target="tpu_custom_call" | custom-call | tf_op jit(solution)/shard_map/pallas_call | solution.py:517
  36.5 1.4 %shard_map.38 = f32[256,2048]{1,0:T(8,128)} custom-call(f32[256,2048]{1,0:T(8,128)S(1)} %get-tuple-element.7.x, f32[8,2048]{1,0:T(8,128)S(1)} %get-tuple-element.8.coarse), custom_call_target="tpu_custom_call" | custom-call | tf_op jit(solution)/shard_map/pallas_call | solution.py:560

commit v3 on v2

--- a/solution.py
+++ b/solution.py
@@ -69,6 +69,20 @@
     ah, al = split(a)
     bh, bl = split(b)
     return dot(ah, bh) + (dot(al, bh) + dot(ah, bl))
+
+
+def packed(tile):
+    return tile[0:4] + pltpu.roll(tile, 64, 1)[4:8]
+
+
+def unpacked(buf):
+    left = iota((4, 128), 1) < 64
+    parts = []
+    for y in range(SIDE):
+        first, second = buf[y], buf[SIDE + y]
+        parts.append(jnp.where(left, first, pltpu.roll(second, 64, 1)))
+        parts.append(jnp.where(left, pltpu.roll(first, 64, 1), second))
+    return jnp.concatenate(parts, axis=0)
 
 
 def correct_kernel(
@@ -166,28 +180,8 @@
     both = pl.ds(0, cols + 128)
     up, down = row > 0, row < last
 
-    whole(ext.at[pl.ds(16, 16), own], edge_sem)
-    pl.semaphore_wait(
-        barrier,
-        7 + 2 * crosses_up.astype(I32) + 2 * crosses_down.astype(I32),
-    )
-
-    @pl.when(up)
-    def _():
-        send(ext.at[first8, own], ext.at[bottom, own], halo_send.at[1], halo_recv.at[1], (stripe, row - 1, col))
-        send(ext.at[first8, inner], ext.at[bottom, pad_there], halo_send.at[1], halo_recv.at[1], (stripe, row - 1, other))
-
-    @pl.when(down)
-    def _():
-        send(ext.at[last8, own], ext.at[top, own], halo_send.at[2], halo_recv.at[2], (stripe, row + 1, col))
-        send(ext.at[last8, inner], ext.at[top, pad_there], halo_send.at[2], halo_recv.at[2], (stripe, row + 1, other))
-
-    for d in (1, 7):
-        signal(ready.at[0], at(px, beside_y(d), col))
-        signal(ready.at[0], at(beside_x(d), py, col))
-
     for i in range(cols // 256):
-        part = (iota((256, 128), 0) + 256 * i) // BS + cells * col
+        part = (iota((256, 128), 0) + 256 * i) // BS
         s1[256 * i : 256 * i + 256, :] = onehot(part == iota((256, 128), 1)).astype(BF16)
     wh, wl = split(taps_of(iota((256, 128), 0) - iota((256, 128), 1) - 64))
     wcat[:, 0:128] = wh
@@ -199,8 +193,28 @@
         part = (iota((128, 128), 0) + 128 * i - 64) // BS
         inside = jnp.logical_and(part >= 0, part < cells)
         s2[128 * i : 128 * i + 128, :] = onehot(
-            jnp.logical_and(inside, part + cells * col == iota((128, 128), 1))
+            jnp.logical_and(inside, part == iota((128, 128), 1))
         ).astype(BF16)
+
+    whole(ext.at[pl.ds(16, 16), own], edge_sem)
+    pl.semaphore_wait(
+        barrier,
+        7 + 2 * crosses_up.astype(I32) + 2 * crosses_down.astype(I32),
+    )
+
+    for d in (1, 7):
+        signal(ready.at[0], at(px, beside_y(d), col))
+        signal(ready.at[0], at(beside_x(d), py, col))
+
+    @pl.when(up)
+    def _():
+        send(ext.at[first8, own], ext.at[bottom, own], halo_send.at[1], halo_recv.at[1], (stripe, row - 1, col))
+        send(ext.at[first8, inner], ext.at[bottom, pad_there], halo_send.at[1], halo_recv.at[1], (stripe, row - 1, other))
+
+    @pl.when(down)
+    def _():
+        send(ext.at[last8, own], ext.at[top, own], halo_send.at[2], halo_recv.at[2], (stripe, row + 1, col))
+        send(ext.at[last8, inner], ext.at[top, pad_there], halo_send.at[2], halo_recv.at[2], (stripe, row + 1, other))
 
     for i in range(8):
         if i % 2 == 0:
@@ -211,24 +225,19 @@
         cb[16 + 32 * i : 48 + 32 * i, 128 : cols + 128] = x.astype(BF16)
     sums = dot_exact(rs[...], s1[...])
     means = sums.reshape(8, 8, 128).sum(axis=1) * (1.0 / (255.0 * BS * BS))
-    mbuf[mine] = means
+    mbuf[mine] = packed(means)
 
     send(ext.at[body, inner], ext.at[body, pad_there], halo_send.at[0], halo_recv.at[0], at(px, py, other))
 
-    pl.semaphore_wait(ready.at[0], 4)
-    for d in (2, 6):
-        signal(ready.at[1], at(px, beside_y(d), col))
-        signal(ready.at[1], at(beside_x(d), py, col))
-
-    def spread_y(buf, sem):
-        for d in ORDER:
+    def spread_y(buf, sem, order, partner):
+        for d in order:
             for c in (0, 1):
                 send(buf.at[mine], buf.at[mine], sem.at[0], sem.at[1], at(px, beside_y(d), c))
-        send(buf.at[mine], buf.at[mine], sem.at[0], sem.at[1], at(px, py, other))
+        if partner:
+            send(buf.at[mine], buf.at[mine], sem.at[0], sem.at[1], at(px, py, other))
 
     def collect_y(buf, sem):
         whole(buf.at[pl.ds(0, 2 * SIDE - 1)], sem.at[1])
-        return (buf[0:SIDE] + buf[SIDE:]).reshape(64, 128)
 
     def spread_x(buf, sem):
         for d in ORDER:
@@ -294,11 +303,18 @@
         result = dot(both, high[here, lanes])
         return result[0:count] + result[count:] + dot(b16[0:count, 0:depth], low[here, lanes])
 
+    pl.semaphore_wait(ready.at[0], 4)
+    for d in (2, 6):
+        signal(ready.at[1], at(px, beside_y(d), col))
+        signal(ready.at[1], at(beside_x(d), py, col))
+
+    spread_y(mbuf, m_sem, (2, 6, 1, 7), True)
     body_rows, edge_rows = ((16, 256),), ((0, 16), (272, 16))
     whole(ext.at[body, pad_here], halo_recv.at[0])
     for pad in (0, cols + 128):
         cb[16:272, pad : pad + 128] = ext[16:272, pad : pad + 128].astype(F32).astype(BF16)
     blur_across(cb, None, hhi, hlo, body_rows, wide // 128)
+
     shift_coverage(body_rows)
 
     tiles = [slice(256 * j, 256 * j + 256) for j in range(wide // 256)]
@@ -322,12 +338,53 @@
         main_rows(lanes)
 
     pl.semaphore_wait(ready.at[1], 4)
-    spread_y(mbuf, m_sem)
-
-    for i in range(wide // 128):
-        cell = (iota((128, 128), 1) + 128 * i + cols * col - 64 + 128) // BS - 4
-        sps[:, 128 * i : 128 * i + 128] = onehot(cell == iota((128, 128), 0)).astype(BF16)
-
+    spread_y(mbuf, m_sem, (4, 3, 5), False)
+
+    part, side = iota((128, 192), 0) // 64, lax.rem(iota((128, 192), 0) // 32, 2)
+    piece = iota((128, 192), 1) // 48
+    value = taps_of(lax.rem(iota((128, 192), 1), 48) - lax.rem(iota((128, 192), 0), 32) - 16 * side)
+    high, low = split(value)
+    value = jnp.where(part == 0, high.astype(F32), jnp.where(lax.rem(piece, 2) == 0, low.astype(F32), 0.0))
+    edge_taps = jnp.where(side == piece // 2, value, 0.0).astype(BF16)
+
+
+    @pl.when(up)
+    def _():
+        whole(ext.at[top, both], halo_recv.at[2])
+
+    @pl.when(down)
+    def _():
+        whole(ext.at[bottom, both], halo_recv.at[1])
+
+    for first in (0, 272):
+        cb[first : first + 16, :] = ext[first : first + 16, :].astype(F32).astype(BF16)
+    blur_across(cb, None, hhi, hlo, edge_rows, wide // 128)
+    shift_coverage(edge_rows)
+    for lanes in tiles:
+        inputs = jnp.concatenate(
+            [hhi[0:48, lanes], hlo[0:48, lanes], hhi[240:288, lanes], hlo[240:288, lanes]], 0
+        )
+        result = dot(edge_taps, inputs)
+        t = 1.5 - (result[0:64] + result[64:128]) * (0.5 / 255.0)
+        tt[0:32, lanes] = t[0:32]
+        tt[256:288, lanes] = t[32:64]
+        product = cs[16:32, lanes] * t[16:32]
+        asum[64:72, lanes] = product[0:8] + product[8:16]
+        product = cs[256:272, lanes] * t[32:48]
+        asum[72:80, lanes] = product[0:8] + product[8:16]
+    sums = dot_exact(asum[...], s2[...]).reshape(10, 8, 128).sum(axis=1)
+    cell_row = iota((8, 128), 0)
+    sums = (
+        sums[0:8]
+        + jnp.where(cell_row == 0, sums[8:9], 0.0)
+        + jnp.where(cell_row == 7, sums[9:10], 0.0)
+    )
+    abuf[mine] = packed(sums * (1.0 / (255.0 * BS * BS)))
+    spread_y(abuf, a_sem, ORDER, True)
+
+    collect_y(mbuf, m_sem)
+    mx = unpacked(mbuf)
+    mext[48:112, :] = mx
     to_region = jnp.where(
         iota((128, 128), 0) // 8 == lax.rem(iota((128, 128), 1), 16), 1.0 / 64.0, 0.0
     ).astype(BF16)
@@ -335,6 +392,13 @@
 
     def region_row(field):
         return jnp.where(own_lanes, dot_exact(field, to_region), 0.0).sum(axis=0, keepdims=True)
+
+    pbuf[px] = region_row(mx)
+    spread_slabs(mext, ms_sem)
+    spread_x(pbuf, p_sem)
+    for i in range(wide // 128):
+        cell = (iota((128, 128), 1) + 128 * i + cols * col - 64 + 128) // BS - 4
+        sps[:, 128 * i : 128 * i + 128] = onehot(cell == iota((128, 128), 0)).astype(BF16)
 
     across = gauss_of(iota((128, 128), 0) - iota((128, 128), 1))
     across = jnp.where(
@@ -369,59 +433,14 @@
     zph, zpl = split(dot_exact(0.2 * zc, sps[:, 64 : cols + 64]))
     zp[0] = zph
     zp[1] = zpl
-    part, side = iota((128, 192), 0) // 64, lax.rem(iota((128, 192), 0) // 32, 2)
-    piece = iota((128, 192), 1) // 48
-    value = taps_of(lax.rem(iota((128, 192), 1), 48) - lax.rem(iota((128, 192), 0), 32) - 16 * side)
-    high, low = split(value)
-    value = jnp.where(part == 0, high.astype(F32), jnp.where(lax.rem(piece, 2) == 0, low.astype(F32), 0.0))
-    edge_taps = jnp.where(side == piece // 2, value, 0.0).astype(BF16)
-
-
-    @pl.when(up)
-    def _():
-        whole(ext.at[top, both], halo_recv.at[2])
-
-    @pl.when(down)
-    def _():
-        whole(ext.at[bottom, both], halo_recv.at[1])
-
-    for first in (0, 272):
-        cb[first : first + 16, :] = ext[first : first + 16, :].astype(F32).astype(BF16)
-    blur_across(cb, None, hhi, hlo, edge_rows, wide // 128)
-    shift_coverage(edge_rows)
-    for lanes in tiles:
-        inputs = jnp.concatenate(
-            [hhi[0:48, lanes], hlo[0:48, lanes], hhi[240:288, lanes], hlo[240:288, lanes]], 0
-        )
-        result = dot(edge_taps, inputs)
-        t = 1.5 - (result[0:64] + result[64:128]) * (0.5 / 255.0)
-        tt[0:32, lanes] = t[0:32]
-        tt[256:288, lanes] = t[32:64]
-        product = cs[16:32, lanes] * t[16:32]
-        asum[64:72, lanes] = product[0:8] + product[8:16]
-        product = cs[256:272, lanes] * t[32:48]
-        asum[72:80, lanes] = product[0:8] + product[8:16]
-    sums = dot_exact(asum[...], s2[...]).reshape(10, 8, 128).sum(axis=1)
-    cell_row = iota((8, 128), 0)
-    sums = (
-        sums[0:8]
-        + jnp.where(cell_row == 0, sums[8:9], 0.0)
-        + jnp.where(cell_row == 7, sums[9:10], 0.0)
-    )
-    abuf[mine] = sums * (1.0 / (255.0 * BS * BS))
-    spread_y(abuf, a_sem)
-
-    mx = collect_y(mbuf, m_sem)
-    mext[48:112, :] = mx
-    pbuf[px] = region_row(mx)
-    spread_x(pbuf, p_sem)
-    spread_slabs(mext, ms_sem)
+
     collect_slabs(mext, ms_sem)
     swept = dot_across(mext[...])
     back_x = dot3(gauss_of(iota((64, 160), 0) - iota((64, 160), 1) + 48), swept)
     back_24 = dot3(gauss_of(iota((24, 160), 0) - iota((24, 160), 1) + 40 + 8 * py), swept)
 
-    ax = collect_y(abuf, a_sem)
+    collect_y(abuf, a_sem)
+    ax = unpacked(abuf)
     bx = ax - 0.3 * back_x * mext[48:112, :]
     bext[48:112, :] = bx
     ebuf[px] = region_row(bx)
@@ -473,14 +492,15 @@
     def _():
         whole(ext.at[bottom, both], halo_send.at[2])
 
-    for sem in (ms_sem, bs_sem):
-        @pl.when(px < SIDE - 1)
-        def _():
-            whole(mext.at[pl.ds(0, 48), :], sem.at[0])
-
-        @pl.when(px > 0)
-        def _():
-            whole(mext.at[pl.ds(112, 48), :], sem.at[1])
+    @pl.when(px < SIDE - 1)
+    def _():
+        whole(mext.at[pl.ds(0, 48), :], ms_sem.at[0])
+        whole(bext.at[pl.ds(0, 48), :], bs_sem.at[0])
+
+    @pl.when(px > 0)
+    def _():
+        whole(mext.at[pl.ds(112, 48), :], ms_sem.at[1])
+        whole(bext.at[pl.ds(112, 48), :], bs_sem.at[1])
 
     collect_slabs(bext, bs_sem)
     means2 = bext[...] - 0.2 * fog_160 * mext[...]
@@ -542,10 +562,10 @@
             pltpu.VMEM((288, 160), BF16),
             pltpu.VMEM((2, 128, cols), BF16),
             pltpu.VMEM((24, wide), F32),
-            pltpu.VMEM((2 * SIDE, 8, 128), F32),
+            pltpu.VMEM((2 * SIDE, 4, 128), F32),
             pltpu.VMEM((160, 128), F32),
             pltpu.VMEM((SIDE, 1, 128), F32),
-            pltpu.VMEM((2 * SIDE, 8, 128), F32),
+            pltpu.VMEM((2 * SIDE, 4, 128), F32),
             pltpu.VMEM((160, 128), F32),
             pltpu.VMEM((SIDE, 1, 128), F32),
             pltpu.VMEM(fog_rows.shape, F32),

time: 38 us -> 37.3 us (0.982)
  Pallas kernels: 37.9 us -> 37.2 us
    pallas_call x1, Pallas kernels: 36.5 us -> 35.8 us  [shards(): pl.pallas_call(correct_kernel, out_shape=(jax.ShapeDtypeStruct((rows, col...]
where the time goes in v3:
time: 37.3 us; the launch traced here: 37.2 us
  Pallas kernels  37.2 us (100%)
    pallas_call x1, Pallas kernels, shards(): pl.pallas_call(correct_kernel, out_shape=(jax.ShapeDtypeStruct((rows, col...  35.8 us
    pallas_call x1, Pallas kernels, shards(): pl.pallas_call(finish_kernel, out_shape=jax.ShapeDtypeStruct((rows, cols)...  1.4 us

profile of v3, /device:TPU:513, one launch (start us, length us, event | category | flops | bytes accessed | tf_op | source)
XLA Modules:
  0.0 37.2 jit_solution(5091901893196865945)
XLA Ops:
  0.0 35.8 %shard_map.37 = (f32[256,2048]{1,0:T(8,128)S(1)}, f32[8,2048]{1,0:T(8,128)S(1)}) custom-call(s32[256,2048]{1,0:T(8,128)} %cov.1, f32[64,64]{1,0:T(8,128)} %fogr.1, f32[16,16]{1,0:T(8,128)} %fogc.1), custom_call_target="tpu_custom_call" | custom-call | tf_op jit(solution)/shard_map/pallas_call | solution.py:537
  35.8 1.4 %shard_map.38 = f32[256,2048]{1,0:T(8,128)} custom-call(f32[256,2048]{1,0:T(8,128)S(1)} %get-tuple-element.7.x, f32[8,2048]{1,0:T(8,128)S(1)} %get-tuple-element.8.coarse), custom_call_target="tpu_custom_call" | custom-call | tf_op jit(solution)/shard_map/pallas_call | solution.py:580

commit v4 on v3

--- a/solution.py
+++ b/solution.py
@@ -459,9 +459,7 @@
     fog_160 = dot3(kr_160, fog_wide[:, 0:128])
     for first, count, place in [(0, 16, 7)] + [(16 + 32 * i, 32, 8 + i) for i in range(8)] + [(272, 16, 16)]:
         here = slice(first, first + count)
-        dose = tt[here, :] - row24[place : place + 1, :]
-        tt[here, :] = dose
-        high, low = split(cs[here, :] * dose)
+        high, low = split(cs[here, :] * (tt[here, :] - row24[place : place + 1, :]))
         qhi[here, :] = high
         qlo[here, :] = low
     blur_across(qhi, qlo, h2hi, h2lo, ((0, 288),), cols // 128)
@@ -505,7 +503,7 @@
     collect_slabs(bext, bs_sem)
     means2 = bext[...] - 0.2 * fog_160 * mext[...]
     back2 = dot3(gauss_of(iota((8, 160), 0) - iota((8, 160), 1) + 48 + 8 * py), dot_across(means2))
-    coarse_out[...] = dot_exact(0.3 * back2, sps[:, 64 : cols + 64])
+    coarse_out[...] = dot_exact(0.3 * back2 + coarse[8:16], sps[:, 64 : cols + 64])
     fog_known = 0.2 * fog_lanes * regions.reshape(8, 128)
     collect_x(ebuf, e_sem)
     fog_mean2 = ebuf[...].reshape(8, 128) - fog_known

time: 37.3 us -> 37.3 us (level)
  no operation moved by 1% of the time
where the time goes in v4:
time: 37.3 us; the launch traced here: 37.1 us
  Pallas kernels  37.1 us (99%)
    pallas_call x1, Pallas kernels, shards(): pl.pallas_call(correct_kernel, out_shape=(jax.ShapeDtypeStruct((rows, col...  35.7 us
    pallas_call x1, Pallas kernels, shards(): pl.pallas_call(finish_kernel, out_shape=jax.ShapeDtypeStruct((rows, cols)...  1.4 us

profile of v4, /device:TPU:513, one launch (start us, length us, event | category | flops | bytes accessed | tf_op | source)
XLA Modules:
  0.0 37.1 jit_solution(4222253576901704398)
XLA Ops:
  0.0 35.7 %shard_map.37 = (f32[256,2048]{1,0:T(8,128)S(1)}, f32[8,2048]{1,0:T(8,128)S(1)}) custom-call(s32[256,2048]{1,0:T(8,128)} %cov.1, f32[64,64]{1,0:T(8,128)} %fogr.1, f32[16,16]{1,0:T(8,128)} %fogc.1), custom_call_target="tpu_custom_call" | custom-call | tf_op jit(solution)/shard_map/pallas_call | solution.py:535
  35.7 1.4 %shard_map.38 = f32[256,2048]{1,0:T(8,128)} custom-call(f32[256,2048]{1,0:T(8,128)S(1)} %get-tuple-element.7.x, f32[8,2048]{1,0:T(8,128)S(1)} %get-tuple-element.8.coarse), custom_call_target="tpu_custom_call" | custom-call | tf_op jit(solution)/shard_map/pallas_call | solution.py:578

commit v5 on v4

--- a/solution.py
+++ b/solution.py
@@ -115,7 +115,7 @@
         pltpu.make_async_copy(
             cov.at[pl.ds(start, stop - start), :],
             ext.at[pl.ds(16 + start, stop - start), own],
-            load_sem.at[i // 2],
+            load_sem,
         ).start()
     fog_loads = [
         pltpu.make_async_copy(fogr, fr, fog_sem.at[0]),
@@ -151,7 +151,7 @@
 
     crosses_up = jnp.logical_and(py == 0, px > 0)
     crosses_down = jnp.logical_and(py == SIDE - 1, px < SIDE - 1)
-    for d in (1, 7):
+    for d in (7, 1):
         for c in (0, 1):
             signal(barrier, at(px, beside_y(d), c))
         signal(barrier, at(beside_x(d), py, col))
@@ -217,9 +217,8 @@
         send(ext.at[last8, inner], ext.at[top, pad_there], halo_send.at[2], halo_recv.at[2], (stripe, row + 1, other))
 
     for i in range(8):
-        if i % 2 == 0:
-            start = spans[i][0]
-            whole(ext.at[pl.ds(16 + start, spans[i + 1][1] - start), own], load_sem.at[i // 2])
+        if i == 0:
+            whole(ext.at[pl.ds(24, 240), own], load_sem)
         x = ext[16 + 32 * i : 48 + 32 * i, 128 : cols + 128].astype(F32)
         rs[8 * i : 8 * i + 8, :] = x.reshape(4, 8, cols).sum(axis=0)
         cb[16 + 32 * i : 48 + 32 * i, 128 : cols + 128] = x.astype(BF16)
@@ -568,7 +567,7 @@
             pltpu.VMEM((SIDE, 1, 128), F32),
             pltpu.VMEM(fog_rows.shape, F32),
             pltpu.VMEM(fog_cols.shape, F32),
-            dma(()), dma((4,)), dma((2,)), dma((3,)), dma((3,)), pltpu.SemaphoreType.REGULAR((2,)),
+            dma(()), dma(()), dma((2,)), dma((3,)), dma((3,)), pltpu.SemaphoreType.REGULAR((2,)),
             dma((2,)), dma((2,)), dma((2,)), dma((2,)), dma((4,)), dma((4,)),
         ],
         compiler_params=pltpu.CompilerParams(

time: 37.3 us -> 37.2 us (level)
  no operation moved by 1% of the time
where the time goes in v5:
time: 37.2 us; the launch traced here: 37.1 us
  Pallas kernels  37.1 us (100%)
    pallas_call x1, Pallas kernels, shards(): pl.pallas_call(correct_kernel, out_shape=(jax.ShapeDtypeStruct((rows, col...  35.7 us
    pallas_call x1, Pallas kernels, shards(): pl.pallas_call(finish_kernel, out_shape=jax.ShapeDtypeStruct((rows, cols)...  1.4 us

profile of v5, /device:TPU:513, one launch (start us, length us, event | category | flops | bytes accessed | tf_op | source)
XLA Modules:
  0.0 37.1 jit_solution(6161427471289260930)
XLA Ops:
  0.0 35.7 %shard_map.37 = (f32[256,2048]{1,0:T(8,128)S(1)}, f32[8,2048]{1,0:T(8,128)S(1)}) custom-call(s32[256,2048]{1,0:T(8,128)} %cov.1, f32[64,64]{1,0:T(8,128)} %fogr.1, f32[16,16]{1,0:T(8,128)} %fogc.1), custom_call_target="tpu_custom_call" | custom-call | tf_op jit(solution)/shard_map/pallas_call | solution.py:534
  35.7 1.4 %shard_map.38 = f32[256,2048]{1,0:T(8,128)} custom-call(f32[256,2048]{1,0:T(8,128)S(1)} %get-tuple-element.7.x, f32[8,2048]{1,0:T(8,128)S(1)} %get-tuple-element.8.coarse), custom_call_target="tpu_custom_call" | custom-call | tf_op jit(solution)/shard_map/pallas_call | solution.py:577
